TPU v7x, 32 devices: a whole 2x2x4 slice. The times are simulated.
32 devices in a mesh: seg: 8 (over z, core), tok: 4 (over y, x).
Axes of the slice: x: 2, y: 2, z: 4, core: 2. Of those that a mesh axis runs over, the one named last changes fastest.
Arguments:
- queries: bfloat16 [2, 8, 2, 5120, 256], P(None, 'seg', None, 'tok'), may hold values from -6 to 6
- key_vectors: bfloat16 [2, 8, 2, 5120, 256], P(None, 'seg', None, 'tok'), may hold values from -6 to 6
- values: bfloat16 [2, 8, 2, 5120, 256], P(None, 'seg', None, 'tok'), may hold values from -6 to 6
- token_rates: float32 [2, 8, 2, 5120], P(None, 'seg', None, 'tok'), may hold values from 0.05 to 3
- fast_weights: float32 [8, 3, 256, 256], P('seg', None, None, 'tok'), may hold values from -0.375 to 0.375
- momenta: float32 [8, 3, 256, 256], P('seg', None, None, 'tok'), may hold values from -3 to 3
- fresh_weights: float32 [3, 256, 256], P(None, None, 'tok'), may hold values from -0.375 to 0.375
- fresh_momenta: float32 [3, 256, 256], P(None, None, 'tok'), may hold values from -3 to 3
Outputs:
- outputs: bfloat16 [2, 8, 2, 5120, 256], P(None, 'seg', None, 'tok')
- final_weights: float32 [8, 3, 256, 256], P('seg', None, None, 'tok')
- final_momenta: float32 [8, 3, 256, 256], P('seg', None, None, 'tok')
All inputs are finite; a program needn't handle non-finite values.
Results may differ from a plain program's by a relative error of at most 0.033.
Values may be sent and summed in bfloat16 or wider, within the bound.
A program may use at most 64 MiB of HBM per device.

v0:
```python
import functools
import jax
import jax.numpy as jnp
from jax import lax
from jax.experimental import pallas as pl
from jax.experimental.pallas import tpu as pltpu
from jax.sharding import PartitionSpec as P

momentum_decay = 0.9
learn_rate = 0.05
epsilon = 1e-06
LANES = 128
UNROLL = 5
MESH = pl.DeviceIdType.MESH
f32 = jnp.float32
bf16 = jnp.bfloat16


def flip(index, mask):
    out, bit = index, 1
    while bit <= mask:
        if mask & bit:
            out = out + bit * (1 - 2 * lax.rem(index // bit, 2))
        bit *= 2
    return out


def sigmoid(x):
    return 0.5 + 0.5 * jnp.tanh(0.5 * x)


def mm(a, b):
    return jnp.dot(a, b, preferred_element_type=f32)


def mm_t(a, b):
    return lax.dot_general(a, b, (((1,), (1,)), ((), ())), preferred_element_type=f32)


def kernel(
    n, segs, steps, blocks, tile,
    k_hbm, v_hbm, q_hbm, rates, w_in, m_in, fw_in, fm_in,
    out_hbm, wstate, mstate,
    kbuf, vbuf, qbuf, obuf, kt, scaled, scaled_t, hid, bgate, bup,
    gsend, grecv, bank, msend, mrecv, sq,
    load_sem, store_sem, gs_sem, gr_sem, os_sem, or_sem, es_sem, er_sem, ms_sem, mr_sem,
    qs_sem, qr_sem,
):
    total = steps * blocks
    rows, head = kbuf.shape[1], kbuf.shape[2]
    width = head // n
    tiles = rows // tile
    order = (1, 0, 2)
    around = tuple(range(n - 1, 0, -1))
    seg = lax.axis_index("seg")
    tok = lax.axis_index("tok")
    first = seg == 0
    last = seg == segs - 1
    peers = [flip(tok, d) for d in range(n)]

    def part(p):
        return pl.ds(pl.multiple_of(p * width, width), width)

    mine = part(tok)

    def to_peer(d):
        return {"seg": seg, "tok": peers[d]}

    down = {"seg": lax.rem(seg + 1, segs), "tok": tok}
    up = {"seg": lax.rem(seg + segs - 1, segs), "tok": tok}

    def rcopy(src, dst, send, recv, device):
        return pltpu.make_async_remote_copy(
            src_ref=src, dst_ref=dst, send_sem=send, recv_sem=recv,
            device_id=device, device_id_type=MESH,
        )

    loads = [[
        pltpu.make_async_copy(src.at[b], dst.at[b], load_sem.at[j, b])
        for b in range(total)
    ] for j, (src, dst) in enumerate(((k_hbm, kbuf), (v_hbm, vbuf), (q_hbm, qbuf)))]

    barrier = pltpu.get_barrier_semaphore()
    for d in range(1, n):
        pl.semaphore_signal(barrier, inc=1, device_id=to_peer(d), device_id_type=MESH)

    @pl.when(jnp.logical_not(last))
    def _():
        pl.semaphore_signal(barrier, inc=1, device_id=down, device_id_type=MESH)

    @pl.when(jnp.logical_not(first))
    def _():
        pl.semaphore_signal(barrier, inc=1, device_id=up, device_id_type=MESH)

    for b in range(total):
        loads[0][b].start()
        loads[1][b].start()
    for b in range(total):
        loads[2][b].start()

    wstate[...] = w_in[...]
    mstate[...] = m_in[...]
    for m in range(3):
        bank[total, m, mine, :] = w_in[m].astype(bf16)
    for s in range(steps):
        drawn = rates[s]
        sums = jnp.sum(drawn * drawn, axis=1, keepdims=True)
        sq[tok, s] = jnp.broadcast_to(sums, (blocks, LANES))

    @pl.when(first)
    def _():
        for s in range(1, steps):
            for m in range(3):
                bank[total + s, m, mine, :] = fw_in[m].astype(bf16)

    neighbours = (seg + segs - 1) // segs + (2 * segs - 2 - seg) // segs
    pl.semaphore_wait(barrier, n - 1 + neighbours)

    def ent_copy(s, d, m):
        place = bank.at[total + s, m, mine, :]
        return rcopy(place, place, es_sem.at[s, d, m], er_sem.at[s, d, m], to_peer(d))

    def sq_copy(d):
        return rcopy(sq.at[tok], sq.at[tok], qs_sem.at[d], qr_sem.at[d], to_peer(d))

    for m in order:
        for d in around:
            ent_copy(0, d, m).start()
    for d in around:
        sq_copy(d).start()

    @pl.when(first)
    def _():
        for s in range(1, steps):
            for m in order:
                for d in around:
                    ent_copy(s, d, m).start()

    def g_copy(b, d, m):
        return rcopy(
            gsend.at[m, part(peers[d]), :], grecv.at[b, d, m],
            gs_sem.at[b, d, m], gr_sem.at[b, d, m], to_peer(d),
        )

    def own_copy(b, d, m):
        place = bank.at[b, m, mine, :]
        return rcopy(place, place, os_sem.at[b, d, m], or_sem.at[b, d, m], to_peer(d))

    def relay_copy(b, s, d, m):
        piece = part(peers[d])
        return rcopy(
            bank.at[b, m, piece, :], bank.at[total + s + 1, m, piece, :],
            es_sem.at[s + 1, d, m], er_sem.at[s + 1, d, m], down,
        )

    def m_copy(s):
        return rcopy(msend.at[s], mrecv.at[s], ms_sem.at[s], mr_sem.at[s], down)

    def prepare(b):
        pltpu.make_async_copy(k_hbm.at[b], kbuf.at[b], load_sem.at[0, b]).wait()
        pltpu.make_async_copy(v_hbm.at[b], vbuf.at[b], load_sem.at[1, b]).wait()
        kt[...] = kbuf[b].T
        s = b // blocks
        row = jnp.broadcast_to(rates[s, pl.ds(b - s * blocks, 1), :], (LANES, rows))
        column = jnp.concatenate([row.T] * (head // LANES), axis=1)
        product = (column * vbuf[b].astype(f32)).astype(bf16)
        scaled[...] = product
        scaled_t[...] = product.T

    def gradients(b, slot):
        w1, w2, w3 = bank[slot, 0], bank[slot, 1], bank[slot, 2]

        @pl.loop(0, tiles, unroll=UNROLL)
        def _(i):
            at = pl.ds(pl.multiple_of(i * tile, tile), tile)
            keys = kbuf[b, at, :]
            back = mm(scaled[at, :], w2)
            gate = mm_t(keys, w1)
            up_pre = mm_t(keys, w3)
            sig = sigmoid(gate)
            act = gate * sig
            slope = sig + act * (1.0 - sig)
            hid[at, :] = (act * up_pre).astype(bf16)
            bgate[at, :] = (back * up_pre * slope).astype(bf16)
            bup[at, :] = (back * act).astype(bf16)

        for m in order:
            if m == 1:
                grad = mm(scaled_t[...], hid[...])
            else:
                grad = mm(kt[...], (bgate if m == 0 else bup)[...]).T
            gsend[m] = grad.astype(bf16)
            for d in around:
                g_copy(b, d, m).start()

    def update(b, m, factor):
        grad = gsend[m, mine, :].astype(f32)
        for d in range(1, n):
            grad = grad + grecv[b, d, m].astype(f32)
        moment = momentum_decay * mstate[m] - grad * factor
        weight = wstate[m]
        stepped = weight - learn_rate * moment
        before = jnp.sum(weight * weight, axis=1, keepdims=True)
        after = jnp.sum(stepped * stepped, axis=1, keepdims=True)
        weight = stepped * jnp.sqrt(before / (after + epsilon))
        mstate[m] = moment
        wstate[m] = weight
        bank[b, m, mine, :] = weight.astype(bf16)

    def apply_fast(b):
        pltpu.make_async_copy(q_hbm.at[b], qbuf.at[b], load_sem.at[2, b]).wait()
        w1, w2, w3 = bank[b, 0], bank[b, 1], bank[b, 2]

        @pl.loop(0, tiles, unroll=UNROLL)
        def _(i):
            at = pl.ds(pl.multiple_of(i * tile, tile), tile)
            asked = qbuf[b, at, :]
            gate = mm_t(asked, w1)
            hidden = (gate * sigmoid(gate) * mm_t(asked, w3)).astype(bf16)
            obuf[b, at, :] = mm_t(hidden, w2).astype(bf16)

        pltpu.make_async_copy(obuf.at[b], out_hbm.at[b], store_sem.at[b]).start()

    prepare(0)
    for d in range(1, n):
        sq_copy(d).wait_recv()

    @pl.loop(0, total)
    def _(b):
        s = b // blocks
        g = b - s * blocks
        inner = (g + blocks - 1) // blocks
        entered = jnp.logical_and(jnp.logical_and(g == 0, s > 0), jnp.logical_not(first))

        @pl.when(g == 0)
        def _():
            for m in order:
                for d in around:
                    ent_copy(s, d, m).wait_recv()

        @pl.when(jnp.logical_and(jnp.logical_and(g == 0, s > 0), first))
        def _():
            wstate[...] = fw_in[...]
            mstate[...] = fm_in[...]

        @pl.when(entered)
        def _():
            for m in order:
                relay_copy(b - 1, s - 1, 0, m).wait_recv()
                wstate[m] = bank[total + s, m, mine, :].astype(f32)

        gradients(b, (total + s) * (1 - inner) + (b - 1) * inner)

        @pl.when(g > 0)
        def _():
            apply_fast(b - 1)

        @pl.when(entered)
        def _():
            m_copy(s - 1).wait_recv()
            mstate[...] = mrecv[s - 1].astype(f32)

        border = jnp.logical_and(g == blocks - 1, s < steps - 1)
        passing = jnp.logical_and(border, jnp.logical_not(last))
        square = sq[0, s, pl.ds(g, 1), :]
        for p in range(1, n):
            square = square + sq[p, s, pl.ds(g, 1), :]
        factor = lax.rsqrt(jnp.concatenate([square] * (head // LANES), axis=1))

        for m in order:
            for d in around:
                g_copy(b, d, m).wait_recv()
            update(b, m, factor)

            @pl.when(passing)
            def _():
                relay_copy(b, s, 0, m).start()

            for d in around:
                own_copy(b, d, m).start()

        @pl.when(passing)
        def _():
            msend[s] = mstate[...].astype(bf16)
            m_copy(s).start()

        for m in order:
            for d in around:
                g_copy(b, d, m).wait_send()

        @pl.when(b < total - 1)
        def _():
            prepare(b + 1)

        for m in order:
            for d in range(1, n):
                own_copy(b, d, m).wait_recv()

                @pl.when(passing)
                def _():
                    relay_copy(b, s, d, m).start()

        @pl.when(g == blocks - 1)
        def _():
            apply_fast(b)

        for m in order:
            for d in around:
                own_copy(b, d, m).wait_send()

        @pl.when(passing)
        def _():
            for m in order:
                for d in range(n):
                    relay_copy(b, s, d, m).wait_send()
            m_copy(s).wait_send()

    for d in around:
        sq_copy(d).wait_send()
        for m in order:
            ent_copy(0, d, m).wait_send()

    @pl.when(first)
    def _():
        for s in range(1, steps):
            for m in order:
                for d in around:
                    ent_copy(s, d, m).wait_send()

    for b in range(total):
        pltpu.make_async_copy(obuf.at[b], out_hbm.at[b], store_sem.at[b]).wait()


def body(n, segs, queries, keys, values, rates, weights, momenta, fresh_w, fresh_m):
    steps, _, blocks, rows, head = queries.shape
    total = steps * blocks
    width = head // n
    tile = 256 if rows % 256 == 0 else rows
    flat = (total, rows, head)
    piece = (3, width, head)
    hbm = pl.BlockSpec(memory_space=pl.ANY)
    vmem = pl.BlockSpec(memory_space=pltpu.VMEM)
    dma = pltpu.SemaphoreType.DMA
    big = (rows, head)
    turned = (head, rows)
    outs = pl.pallas_call(
        functools.partial(kernel, n, segs, steps, blocks, tile),
        out_shape=(
            jax.ShapeDtypeStruct(flat, bf16),
            jax.ShapeDtypeStruct(piece, f32),
            jax.ShapeDtypeStruct(piece, f32),
        ),
        in_specs=[hbm, hbm, hbm, vmem, vmem, vmem, vmem, vmem],
        out_specs=(hbm, vmem, vmem),
        scratch_shapes=[pltpu.VMEM(flat, bf16)] * 4
        + [
            pltpu.VMEM(turned, bf16),
            pltpu.VMEM(big, bf16),
            pltpu.VMEM(turned, bf16),
            pltpu.VMEM(big, bf16),
            pltpu.VMEM(big, bf16),
            pltpu.VMEM(big, bf16),
            pltpu.VMEM((3, head, head), bf16),
            pltpu.VMEM((total, n) + piece, bf16),
            pltpu.VMEM((total + steps, 3, head, head), bf16),
            pltpu.VMEM((steps,) + piece, bf16),
            pltpu.VMEM((steps,) + piece, bf16),
            pltpu.VMEM((n, steps, blocks, LANES), f32),
            dma((3, total)),
            dma((total,)),
            dma((total, n, 3)),
            dma((total, n, 3)),
            dma((total, n, 3)),
            dma((total, n, 3)),
            dma((steps, n, 3)),
            dma((steps, n, 3)),
            dma((steps,)),
            dma((steps,)),
            dma((n,)),
            dma((n,)),
        ],
        compiler_params=pltpu.CompilerParams(
            collective_id=0, has_side_effects=True, vmem_limit_bytes=60 * 1024 * 1024
        ),
    )(
        keys.reshape(flat), values.reshape(flat), queries.reshape(flat), rates[:, 0],
        jnp.swapaxes(weights[0], 1, 2), jnp.swapaxes(momenta[0], 1, 2),
        jnp.swapaxes(fresh_w, 1, 2), jnp.swapaxes(fresh_m, 1, 2),
    )
    return (
        outs[0].reshape(queries.shape),
        jnp.swapaxes(outs[1], 1, 2)[None],
        jnp.swapaxes(outs[2], 1, 2)[None],
    )


def solution(mesh):
    n, segs = mesh.shape["tok"], mesh.shape["seg"]
    return jax.shard_map(
        functools.partial(body, n, segs),
        mesh=mesh,
        in_specs=(
            P(None, "seg", None, "tok", None),
            P(None, "seg", None, "tok", None),
            P(None, "seg", None, "tok", None),
            P(None, "seg", None, "tok"),
            P("seg", None, None, "tok"),
            P("seg", None, None, "tok"),
            P(None, None, "tok"),
            P(None, None, "tok"),
        ),
        out_specs=(
            P(None, "seg", None, "tok", None),
            P("seg", None, None, "tok"),
            P("seg", None, None, "tok"),
        ),
        check_vma=False,
    )
```

profile of v0, /device:TPU:0, one launch (start us, length us, event | category | flops | bytes accessed | tf_op | source)
XLA Modules:
  0.0 69.9 jit_solution(2208706062078833167)
XLA Ops:
  0.6 64.5 %shard_map.103 = (bf16[4,1280,256]{2,1,0:T(8,128)(2,1)}, f32[3,64,256]{2,1,0:T(8,128)}, f32[3,64,256]{2,1,0:T(8,128)}) custom-call(bf16[4,1280,256]{2,1,0:T(8,128)(2,1)} %bitcast.22, bf16[4,1280,256]{2,1,0:T(8,128)(2,1)} %bitcast.23, bf16[4,1280,256]{2,1,0:T(8,128)(2,1)} %bitcast.24, f32[2,2,1280]{2,1,0:T(2,128)} %bitcast.31, f32[3,64,256]{2,1,0:T(8,128)} %bitcast.27, ...), custom_call_target="tpu_custom_call" | custom-call | tf_op jit(solution)/shard_map/pallas_call | solution.py:346
  65.1 0.0 copy-start.1
  65.1 0.0 copy-start
  65.1 3.4 %copy.15 = bf16[2,1,2,1280,256]{4,3,2,1,0:T(8,128)(2,1)} copy(bf16[2,1,2,1280,256]{4,3,2,1,0:T(8,128)(2,1)} %bitcast.21) | data formatting | bytes 5242880
  68.6 0.0 copy-done.1
  68.6 0.7 copy.16
  69.2 0.0 copy-done
  69.2 0.7 copy.17
Async XLA Ops:
  65.1 3.5 %copy-start.1 = (f32[3,64,256]{2,1,0:T(8,128)S(1)}, f32[3,64,256]{2,1,0:T(8,128)}, u32[]{:S(2)}) copy-start(f32[3,64,256]{2,1,0:T(8,128)} %get-tuple-element.7) | copy-start | bytes 589828
  65.1 4.1 %copy-start = (f32[3,64,256]{2,1,0:T(8,128)S(1)}, f32[3,64,256]{2,1,0:T(8,128)}, u32[]{:S(2)}) copy-start(f32[3,64,256]{2,1,0:T(8,128)} %get-tuple-element.8) | copy-start | bytes 589828
where the time goes:
time: 70.1 us; the launch traced here: 69.9 us
  Pallas kernels  64.5 us (92%)
  local copies, waits for them, and re-layouts  4.81 us (7%)
    pallas_call x1, Pallas kernels, body(): pl.pallas_call(functools.partial(kernel, n, segs, steps, blocks, tile), o...  64.5 us
    unnamed x7, local copies, waits for them, and re-layouts  4.81 us

commit v1 on v0

--- a/solution.py
+++ b/solution.py
@@ -331,6 +331,526 @@
         pltpu.make_async_copy(obuf.at[b], out_hbm.at[b], store_sem.at[b]).wait()
 
 
+def quad_kernel(
+    segs, steps, blocks, tile,
+    k_hbm, v_hbm, q_hbm, rates, w_in, m_in, fw_in, fm_in,
+    out_hbm, w_out, m_out,
+    kbuf, vbuf, qbuf, obuf, kt, scaled, scaled_t, hid, bgu,
+    bank13, bank2, gs13, gs2, got, mid, wst, mst,
+    mx, mr, msend, mrecv, sq, sq_in,
+    load_sem, store_sem, st_s, st_r, en_s, en_r, rl_s, rl_r, mm_s, mm_r, mx_s, mx_r, qs, qr,
+):
+    total = steps * blocks
+    rows, head = kbuf.shape[1], kbuf.shape[2]
+    unit = head // 8
+    half = head // 2
+    tiles = rows // tile
+    seg = lax.axis_index("seg")
+    tok = lax.axis_index("tok")
+    inner = lax.rem(tok, 2)
+    outer = tok // 2
+    first = seg == 0
+    last = seg == segs - 1
+    own = (inner, outer)
+    far = (1 - inner, 1 - outer)
+    near_in = {"seg": seg, "tok": 2 * outer + (1 - inner)}
+    near_out = {"seg": seg, "tok": 2 * (1 - outer) + inner}
+    gather_to = (near_in, near_out)
+    cross_to = (near_out, near_in)
+    down = {"seg": lax.rem(seg + 1, segs), "tok": tok}
+    up = {"seg": lax.rem(seg + segs - 1, segs), "tok": tok}
+
+    def rcopy(src, dst, send, recv, device):
+        return pltpu.make_async_remote_copy(
+            src_ref=src, dst_ref=dst, send_sem=send, recv_sem=recv,
+            device_id=device, device_id_type=MESH,
+        )
+
+    def place(slot, item, p, s):
+        if item < 2:
+            return bank13.at[slot, item, :, s, p]
+        return bank2.at[slot, :, s, 0] if p == 0 else bank2.at[slot, s, :, 1]
+
+    def load_place(slot, item, p, s):
+        return place(slot, item, p, s)[...]
+
+    def grad_place(b, item, p, s):
+        if item < 2:
+            return gs13.at[b, item, :, s, p]
+        return gs2.at[b, :, s, 0] if p == 0 else gs2.at[b, s, :, 1]
+
+    def swap(x):
+        block = lax.broadcasted_iota(jnp.int32, x.shape, 1) // unit
+        ahead = pltpu.roll(x, 2 * unit, 1)
+        behind = pltpu.roll(x, head - 2 * unit, 1)
+        return jnp.where(block == 5, ahead, jnp.where(block == 3, behind, x))
+
+    barrier = pltpu.get_barrier_semaphore()
+    for peer in (near_in, near_out):
+        pl.semaphore_signal(barrier, inc=1, device_id=peer, device_id_type=MESH)
+
+    @pl.when(jnp.logical_not(last))
+    def _():
+        pl.semaphore_signal(barrier, inc=1, device_id=down, device_id_type=MESH)
+
+    @pl.when(jnp.logical_not(first))
+    def _():
+        pl.semaphore_signal(barrier, inc=1, device_id=up, device_id_type=MESH)
+
+    loads = [[
+        pltpu.make_async_copy(src.at[b], dst.at[b], load_sem.at[j, b])
+        for b in range(total)
+    ] for j, (src, dst) in enumerate(((k_hbm, kbuf), (v_hbm, vbuf), (q_hbm, qbuf)))]
+    for b in range(total):
+        loads[0][b].start()
+        loads[1][b].start()
+    for b in range(total):
+        loads[2][b].start()
+
+    def fill_bank(e, source):
+        for k, m in enumerate((0, 2)):
+            bank13[e, outer, k, inner, 0] = source[m, :unit, :].astype(bf16)
+            bank13[e, inner, k, outer, 1] = source[m, unit:, :].astype(bf16)
+        for h in range(2):
+            bank2[e, outer, inner, h] = swap(source[1, h * unit:(h + 1) * unit, :]).astype(bf16)
+
+    def fill_moments(s, source):
+        for h in range(2):
+            at = slice(h * unit, (h + 1) * unit)
+            mx[s, h, 0] = source[0, at, :].astype(bf16)
+            mx[s, h, 1] = source[2, at, :].astype(bf16)
+            mx[s, h, 2] = swap(source[1, at, :]).astype(bf16)
+
+    def fill_state(ref, source):
+        for k, m in enumerate((0, 2)):
+            ref[outer, 0, k] = source[m, :unit, :]
+            ref[inner, 1, k] = source[m, unit:, :]
+        ref[2, 0, outer] = swap(source[1, :unit, :])
+        ref[2, 1, inner] = swap(source[1, unit:, :])
+
+    fill_bank(total, w_in)
+    for s in range(steps):
+        drawn = rates[s]
+        sums = jnp.sum(drawn * drawn, axis=1, keepdims=True)
+        sq[0, s] = jnp.broadcast_to(sums, (blocks, LANES))
+
+    def entry_copies(s):
+        e = total + s
+        out = []
+        for d, peer in enumerate((near_in, near_out)):
+            pieces = (
+                bank13.at[e, outer, :, inner, 0],
+                bank13.at[e, inner, :, outer, 1],
+                bank2.at[e, outer, inner],
+            )
+            for j, piece in enumerate(pieces):
+                out.append(rcopy(piece, piece, en_s.at[s, d, j], en_r.at[s, d, j], peer))
+        return out
+
+    def forward_copies(s):
+        e = total + s
+        pieces = (
+            (bank13.at[e, 1 - outer, :, inner, 0], bank2.at[e, 1 - outer, inner, 0]),
+            (bank13.at[e, 1 - inner, :, outer, 1], bank2.at[e, outer, 1 - inner, 1]),
+        )
+        return [[
+            rcopy(piece, piece, en_s.at[s, d, 3 + j], en_r.at[s, d, 3 + j], peer)
+            for j, piece in enumerate(pieces[d])
+        ] for d, peer in enumerate((near_in, near_out))]
+
+    def moment_copies(s):
+        return [
+            rcopy(mx.at[s, h], mr.at[s, h], mx_s.at[s, h], mx_r.at[s, h], cross_to[h])
+            for h in range(2)
+        ]
+
+    def start_entry(s):
+        for copy in entry_copies(s):
+            copy.start()
+
+    def pass_entry(s):
+        sent, onward = entry_copies(s), forward_copies(s)
+        sent[3].wait_recv()
+        onward[0][0].start()
+        sent[1].wait_recv()
+        onward[1][0].start()
+        sent[5].wait_recv()
+        onward[0][1].start()
+        sent[2].wait_recv()
+        onward[1][1].start()
+        sent[0].wait_recv()
+        sent[4].wait_recv()
+
+    def take_entry(s):
+        for pair in forward_copies(s):
+            for copy in pair:
+                copy.wait_recv()
+
+    def take_state(s, weights, moments):
+        e = total + s
+        fill_state(wst, weights)
+        fill_state(mst, moments)
+        wst[1 - outer, 0] = bank13[e, 1 - outer, :, inner, 0].astype(f32)
+        wst[1 - inner, 1] = bank13[e, 1 - inner, :, outer, 1].astype(f32)
+        wst[2, 0, 1 - outer] = bank2[e, 1 - outer, inner, 0].astype(f32)
+        wst[2, 1, 1 - inner] = bank2[e, outer, 1 - inner, 1].astype(f32)
+        for copy in moment_copies(s):
+            copy.wait_recv()
+        mst[1 - outer, 0] = mr[s, 0, :2].astype(f32)
+        mst[1 - inner, 1] = mr[s, 1, :2].astype(f32)
+        mst[2, 0, 1 - outer] = mr[s, 0, 2].astype(f32)
+        mst[2, 1, 1 - inner] = mr[s, 1, 2].astype(f32)
+
+    def square_copy(j):
+        return rcopy(sq.at[j], sq_in.at[j], qs.at[j], qr.at[j], (near_in, near_out)[j])
+
+    neighbours = (seg + segs - 1) // segs + (2 * segs - 2 - seg) // segs
+    pl.semaphore_wait(barrier, 2 + neighbours)
+    start_entry(0)
+    square_copy(0).start()
+
+    fill_moments(0, m_in)
+    for copy in moment_copies(0):
+        copy.start()
+
+    @pl.when(first)
+    def _():
+        for s in range(1, steps):
+            fill_bank(total + s, fw_in)
+            fill_moments(s, fm_in)
+
+    def prepare_keys(b):
+        pltpu.make_async_copy(k_hbm.at[b], kbuf.at[b], load_sem.at[0, b]).wait()
+        kt[...] = kbuf[b].T
+
+    def prepare_values(b):
+        pltpu.make_async_copy(v_hbm.at[b], vbuf.at[b], load_sem.at[1, b]).wait()
+        s = b // blocks
+        row = jnp.broadcast_to(rates[s, pl.ds(b - s * blocks, 1), :], (LANES, rows))
+        column = jnp.concatenate([row.T] * (head // LANES), axis=1)
+        product = (column * vbuf[b].astype(f32)).astype(bf16)
+        scaled[...] = product
+        scaled_t[...] = product.T
+
+    def stage_copy(b, stage, item, p):
+        if stage == 0:
+            src, dst, peer = grad_place(b, item, p, far[p]), got.at[b, 0, item, p], gather_to[p]
+        elif stage == 1:
+            src, dst, peer = mid.at[b, item, p], got.at[b, 1, item, p], cross_to[p]
+        else:
+            src = place(b, item, p, own[p])
+            dst, peer = src, gather_to[p]
+        return rcopy(src, dst, st_s.at[b, stage, item, p], st_r.at[b, stage, item, p], peer)
+
+    def relay_copy(b, s, item, j):
+        p = j % 2
+        piece = own[p] if j < 2 else far[p]
+        return rcopy(
+            place(b, item, p, piece), place(total + s + 1, item, p, piece),
+            rl_s.at[s, item, j], rl_r.at[s, item, j], down,
+        )
+
+    def m_copy(s):
+        return rcopy(msend.at[s], mrecv.at[s], mm_s.at[s], mm_r.at[s], down)
+
+    def flow(b, slot, c):
+        w13 = bank13[slot, c].reshape(head, head)
+        w2 = bank2[slot].reshape(head, head)[:, c * half:(c + 1) * half]
+
+        @pl.loop(0, tiles, unroll=UNROLL)
+        def _(i):
+            at = pl.ds(pl.multiple_of(i * tile, tile), tile)
+            both = mm_t(kbuf[b, at, :], w13)
+            back = mm(scaled[at, :], w2)
+            gate, up_pre = both[:, :half], both[:, half:]
+            sig = sigmoid(gate)
+            act = gate * sig
+            slope = sig + act * (1.0 - sig)
+            hid[at, c * half:(c + 1) * half] = (act * up_pre).astype(bf16)
+            bgu[c, at, :half] = (back * up_pre * slope).astype(bf16)
+            bgu[c, at, half:] = (back * act).astype(bf16)
+
+    def send_grads(b, item):
+        if item < 2:
+            grad = mm(kt[...], bgu[item]).T.astype(bf16)
+            gs13[b, item] = grad.reshape(gs13.shape[2:])
+        else:
+            gs2[b] = mm(scaled_t[...], hid[...]).astype(bf16).reshape(gs2.shape[1:])
+        for p in range(2):
+            stage_copy(b, 0, item, p).start()
+
+    def pair_sum(b, item):
+        for p in range(2):
+            stage_copy(b, 0, item, p).wait_recv()
+            mine = grad_place(b, item, p, own[p])[...].astype(f32)
+            mid[b, item, p] = (mine + got[b, 0, item, p].astype(f32)).astype(bf16)
+            stage_copy(b, 1, item, p).start()
+
+    def update(b, item, factor):
+        for p in range(2):
+            stage_copy(b, 1, item, p).wait_recv()
+            grad = mid[b, item, p].astype(f32) + got[b, 1, item, p].astype(f32)
+            moment = momentum_decay * mst[item, p] - grad * factor
+            weight = wst[item, p]
+            stepped = weight - learn_rate * moment
+            before = jnp.sum(weight * weight, axis=2, keepdims=True)
+            after = jnp.sum(stepped * stepped, axis=2, keepdims=True)
+            weight = stepped * jnp.sqrt(before / (after + epsilon))
+            mst[item, p] = moment
+            wst[item, p] = weight
+            place(b, item, p, own[p])[...] = weight.astype(bf16)
+            stage_copy(b, 2, item, p).start()
+
+    def apply_fast(b, start, stop):
+        if start == 0:
+            pltpu.make_async_copy(q_hbm.at[b], qbuf.at[b], load_sem.at[2, b]).wait()
+        wa = bank13[b, 0].reshape(head, head)
+        wb = bank13[b, 1].reshape(head, head)
+        w2 = bank2[b].reshape(head, head)
+
+        @pl.loop(start, stop, unroll=min(UNROLL, stop - start))
+        def _(i):
+            at = pl.ds(pl.multiple_of(i * tile, tile), tile)
+            asked = qbuf[b, at, :]
+            parts = []
+            for w13 in (wa, wb):
+                both = mm_t(asked, w13)
+                gate = both[:, :half]
+                parts.append((gate * sigmoid(gate) * both[:, half:]).astype(bf16))
+            obuf[b, at, :] = mm_t(jnp.concatenate(parts, axis=1), w2).astype(bf16)
+
+        if stop == tiles:
+            pltpu.make_async_copy(obuf.at[b], out_hbm.at[b], store_sem.at[b]).start()
+
+    prepare_keys(0)
+    prepare_values(0)
+    pass_entry(0)
+    square_copy(0).wait_recv()
+    sq[1] = sq[0] + sq_in[0]
+    square_copy(1).start()
+
+    @pl.when(first)
+    def _():
+        for s in range(1, steps):
+            start_entry(s)
+            for copy in moment_copies(s):
+                copy.start()
+
+    take_entry(0)
+    cut = (tiles + 1) // 2
+
+    @pl.loop(0, total)
+    def _(b):
+        s = b // blocks
+        g = b - s * blocks
+        inside = (g + blocks - 1) // blocks
+        slot = (total + s) * (1 - inside) + (b - 1) * inside
+        entered = jnp.logical_and(jnp.logical_and(g == 0, s > 0), jnp.logical_not(first))
+        renewed = jnp.logical_and(jnp.logical_and(g == 0, s > 0), first)
+        border = jnp.logical_and(g == blocks - 1, s < steps - 1)
+        passing = jnp.logical_and(border, jnp.logical_not(last))
+
+        @pl.when(renewed)
+        def _():
+            take_entry(s)
+
+        @pl.when(entered)
+        def _():
+            for item in (0, 2):
+                for j in range(4):
+                    relay_copy(b - 1, s - 1, item, j).wait_recv()
+
+        flow(b, slot, 0)
+        send_grads(b, 0)
+
+        @pl.when(g > 0)
+        def _():
+            for p in range(2):
+                stage_copy(b - 1, 2, 1, p).wait_recv()
+
+        @pl.when(entered)
+        def _():
+            for j in range(4):
+                relay_copy(b - 1, s - 1, 1, j).wait_recv()
+
+        flow(b, slot, 1)
+        send_grads(b, 2)
+        send_grads(b, 1)
+
+        @pl.when(jnp.logical_and(g == 0, s == 0))
+        def _():
+            square_copy(1).wait_recv()
+            sq[2] = sq[1] + sq_in[1]
+            take_state(0, w_in, m_in)
+
+        @pl.when(renewed)
+        def _():
+            take_state(s, fw_in, fm_in)
+
+        @pl.when(entered)
+        def _():
+            m_copy(s - 1).wait_recv()
+            mst[...] = mrecv[s - 1].astype(f32)
+            for item in range(3):
+                for p in range(2):
+                    wst[item, p] = load_place(total + s, item, p, own[p]).astype(f32)
+
+        square = sq[2, s, pl.ds(g, 1), :]
+        factor = lax.rsqrt(jnp.concatenate([square] * (head // LANES), axis=1))
+
+        @pl.when(g > 0)
+        def _():
+            apply_fast(b - 1, 0, cut)
+
+        pair_sum(b, 0)
+
+        @pl.when(g > 0)
+        def _():
+            apply_fast(b - 1, cut, tiles)
+
+        pair_sum(b, 2)
+        pair_sum(b, 1)
+
+        @pl.when(b < total - 1)
+        def _():
+            prepare_keys(b + 1)
+
+        @pl.when(jnp.logical_and(first, jnp.logical_and(b == 0, steps > 1)))
+        def _():
+            for step in range(1, steps):
+                pass_entry(step)
+
+        update(b, 0, factor)
+
+        @pl.when(passing)
+        def _():
+            for j in range(2):
+                relay_copy(b, s, 0, j).start()
+
+        @pl.when(b < total - 1)
+        def _():
+            prepare_values(b + 1)
+
+        for item in (2, 1):
+            update(b, item, factor)
+
+            @pl.when(passing)
+            def _():
+                for j in range(2):
+                    relay_copy(b, s, item, j).start()
+
+        for item in (0, 2):
+            for p in range(2):
+                stage_copy(b, 2, item, p).wait_recv()
+
+                @pl.when(passing)
+                def _():
+                    relay_copy(b, s, item, 2 + p).start()
+
+        @pl.when(g == blocks - 1)
+        def _():
+            for p in range(2):
+                stage_copy(b, 2, 1, p).wait_recv()
+
+        @pl.when(passing)
+        def _():
+            for p in range(2):
+                relay_copy(b, s, 1, 2 + p).start()
+            msend[s] = mst[...].astype(bf16)
+            m_copy(s).start()
+
+        @pl.when(g == blocks - 1)
+        def _():
+            apply_fast(b, 0, tiles)
+
+    for k, m in enumerate((0, 2)):
+        for ref, state in ((w_out, wst), (m_out, mst)):
+            ref[m, :unit, :] = state[outer, 0, k]
+            ref[m, unit:, :] = state[inner, 1, k]
+    for ref, state in ((w_out, wst), (m_out, mst)):
+        ref[1, :unit, :] = swap(state[2, 0, outer])
+        ref[1, unit:, :] = swap(state[2, 1, inner])
+
+    def drain_entry(s):
+        for copy in entry_copies(s):
+            copy.wait_send()
+        for pair in forward_copies(s):
+            for copy in pair:
+                copy.wait_send()
+        for copy in moment_copies(s):
+            copy.wait_send()
+
+    drain_entry(0)
+
+    @pl.when(first)
+    def _():
+        for s in range(1, steps):
+            drain_entry(s)
+
+    for j in range(2):
+        square_copy(j).wait_send()
+
+    @pl.when(jnp.logical_not(last))
+    def _():
+        for s in range(steps - 1):
+            for item in range(3):
+                for j in range(4):
+                    relay_copy(s * blocks + blocks - 1, s, item, j).wait_send()
+            m_copy(s).wait_send()
+
+    @pl.loop(0, total)
+    def _(b):
+        for stage in range(3):
+            for item in range(3):
+                for p in range(2):
+                    stage_copy(b, stage, item, p).wait_send()
+        pltpu.make_async_copy(obuf.at[b], out_hbm.at[b], store_sem.at[b]).wait()
+
+
+def quad_scratch(steps, blocks, rows, head):
+    total = steps * blocks
+    unit = head // 8
+    flat = (total, rows, head)
+    pair = (2, unit, head)
+    dma = pltpu.SemaphoreType.DMA
+    vmem = pltpu.VMEM
+    return [vmem(flat, bf16)] * 4 + [
+        vmem((head, rows), bf16),
+        vmem((rows, head), bf16),
+        vmem((head, rows), bf16),
+        vmem((rows, head), bf16),
+        vmem((2, rows, head), bf16),
+        vmem((total + steps, 2, 2, 2, 2, unit, head), bf16),
+        vmem((total + steps, 2, 2, 2, unit, head), bf16),
+        vmem((total, 2, 2, 2, 2, unit, head), bf16),
+        vmem((total, 2, 2, 2, unit, head), bf16),
+        vmem((total, 2, 3, 2) + pair, bf16),
+        vmem((total, 3, 2) + pair, bf16),
+        vmem((3, 2) + pair, f32),
+        vmem((3, 2) + pair, f32),
+        vmem((steps, 2, 3, unit, head), bf16),
+        vmem((steps, 2, 3, unit, head), bf16),
+        vmem((steps, 3, 2) + pair, bf16),
+        vmem((steps, 3, 2) + pair, bf16),
+        vmem((3, steps, blocks, LANES), f32),
+        vmem((2, steps, blocks, LANES), f32),
+        dma((3, total)),
+        dma((total,)),
+        dma((total, 3, 3, 2)),
+        dma((total, 3, 3, 2)),
+        dma((steps, 2, 5)),
+        dma((steps, 2, 5)),
+        dma((steps, 3, 4)),
+        dma((steps, 3, 4)),
+        dma((steps,)),
+        dma((steps,)),
+        dma((steps, 2)),
+        dma((steps, 2)),
+        dma((2,)),
+        dma((2,)),
+    ]
+
+
 def body(n, segs, queries, keys, values, rates, weights, momenta, fresh_w, fresh_m):
     steps, _, blocks, rows, head = queries.shape
     total = steps * blocks
@@ -343,17 +863,12 @@
     dma = pltpu.SemaphoreType.DMA
     big = (rows, head)
     turned = (head, rows)
-    outs = pl.pallas_call(
-        functools.partial(kernel, n, segs, steps, blocks, tile),
-        out_shape=(
-            jax.ShapeDtypeStruct(flat, bf16),
-            jax.ShapeDtypeStruct(piece, f32),
-            jax.ShapeDtypeStruct(piece, f32),
-        ),
-        in_specs=[hbm, hbm, hbm, vmem, vmem, vmem, vmem, vmem],
-        out_specs=(hbm, vmem, vmem),
-        scratch_shapes=[pltpu.VMEM(flat, bf16)] * 4
-        + [
+    if n == 4 and head % 256 == 0:
+        run = functools.partial(quad_kernel, segs, steps, blocks, tile)
+        scratch = quad_scratch(steps, blocks, rows, head)
+    else:
+        run = functools.partial(kernel, n, segs, steps, blocks, tile)
+        scratch = [pltpu.VMEM(flat, bf16)] * 4 + [
             pltpu.VMEM(turned, bf16),
             pltpu.VMEM(big, bf16),
             pltpu.VMEM(turned, bf16),
@@ -378,7 +893,17 @@
             dma((steps,)),
             dma((n,)),
             dma((n,)),
-        ],
+        ]
+    outs = pl.pallas_call(
+        run,
+        out_shape=(
+            jax.ShapeDtypeStruct(flat, bf16),
+            jax.ShapeDtypeStruct(piece, f32),
+            jax.ShapeDtypeStruct(piece, f32),
+        ),
+        in_specs=[hbm, hbm, hbm, vmem, vmem, vmem, vmem, vmem],
+        out_specs=(hbm, vmem, vmem),
+        scratch_shapes=scratch,
         compiler_params=pltpu.CompilerParams(
             collective_id=0, has_side_effects=True, vmem_limit_bytes=60 * 1024 * 1024
         ),

time: 70.1 us -> 70 us (level)
  no operation moved by 1% of the time
where the time goes in v1:
time: 70 us; the launch traced here: 69.8 us
  Pallas kernels  64.4 us (92%)
  local copies, waits for them, and re-layouts  4.81 us (7%)
    pallas_call x1, Pallas kernels, body(): pl.pallas_call(run, out_shape=(jax.ShapeDtypeStruct(flat, bf16), jax.Shap...  64.4 us
    unnamed x7, local copies, waits for them, and re-layouts  4.81 us

profile of v1, /device:TPU:0, one launch (start us, length us, event | category | flops | bytes accessed | tf_op | source)
XLA Modules:
  0.0 69.8 jit_solution(1192044204941089477)
XLA Ops:
  0.6 64.4 %shard_map.103 = (bf16[4,1280,256]{2,1,0:T(8,128)(2,1)}, f32[3,64,256]{2,1,0:T(8,128)}, f32[3,64,256]{2,1,0:T(8,128)}) custom-call(bf16[4,1280,256]{2,1,0:T(8,128)(2,1)} %bitcast.22, bf16[4,1280,256]{2,1,0:T(8,128)(2,1)} %bitcast.23, bf16[4,1280,256]{2,1,0:T(8,128)(2,1)} %bitcast.24, f32[2,2,1280]{2,1,0:T(2,128)} %bitcast.31, f32[3,64,256]{2,1,0:T(8,128)} %bitcast.27, ...), custom_call_target="tpu_custom_call" | custom-call | tf_op jit(solution)/shard_map/pallas_call | solution.py:897
  65.0 0.0 copy-start.1
  65.0 0.0 copy-start
  65.0 3.4 %copy.15 = bf16[2,1,2,1280,256]{4,3,2,1,0:T(8,128)(2,1)} copy(bf16[2,1,2,1280,256]{4,3,2,1,0:T(8,128)(2,1)} %bitcast.21) | data formatting | bytes 5242880
  68.5 0.0 copy-done.1
  68.5 0.7 copy.16
  69.1 0.0 copy-done
  69.1 0.7 copy.17
Async XLA Ops:
  65.0 3.5 %copy-start.1 = (f32[3,64,256]{2,1,0:T(8,128)S(1)}, f32[3,64,256]{2,1,0:T(8,128)}, u32[]{:S(2)}) copy-start(f32[3,64,256]{2,1,0:T(8,128)} %get-tuple-element.7) | copy-start | bytes 589828
  65.0 4.1 %copy-start = (f32[3,64,256]{2,1,0:T(8,128)S(1)}, f32[3,64,256]{2,1,0:T(8,128)}, u32[]{:S(2)}) copy-start(f32[3,64,256]{2,1,0:T(8,128)} %get-tuple-element.8) | copy-start | bytes 589828

commit v2 on v0

--- a/solution.py
+++ b/solution.py
@@ -331,6 +331,426 @@
         pltpu.make_async_copy(obuf.at[b], out_hbm.at[b], store_sem.at[b]).wait()
 
 
+def quad_kernel(
+    segs, steps, blocks, tile,
+    k_hbm, v_hbm, q_hbm, rates_hbm, w_hbm, m_hbm, fw_hbm, fm_hbm,
+    out_hbm, w_out, m_out,
+    kbuf, vbuf, qbuf, obuf, kt, scaled, scaled_t, hid, bgu,
+    bank, gs, got, mid, wst, mst,
+    w_in, m_in, fw_in, fm_in, rates, mx, mr, msend, mrecv, sq,
+    load_sem, store_sem, in_sem, st_s, st_r, en_s, en_r, rl_s, rl_r, mm_s, mm_r, mx_s, mx_r, qs, qr,
+):
+    total = steps * blocks
+    n = 4
+    rows, head = kbuf.shape[1], kbuf.shape[2]
+    half = head // 2
+    tiles = rows // tile
+    seg = lax.axis_index("seg")
+    tok = lax.axis_index("tok")
+    inner = lax.rem(tok, 2)
+    outer = tok // 2
+    first = seg == 0
+    last = seg == segs - 1
+    peers = [flip(tok, d) for d in range(n)]
+
+    def to_peer(d):
+        return {"seg": seg, "tok": peers[d]}
+
+    stage_to = ((to_peer(1), to_peer(2)), (to_peer(2), to_peer(1)))
+    down = {"seg": lax.rem(seg + 1, segs), "tok": tok}
+    up = {"seg": lax.rem(seg + segs - 1, segs), "tok": tok}
+
+    def rcopy(src, dst, send, recv, device):
+        return pltpu.make_async_remote_copy(
+            src_ref=src, dst_ref=dst, send_sem=send, recv_sem=recv,
+            device_id=device, device_id_type=MESH,
+        )
+
+    barrier = pltpu.get_barrier_semaphore()
+    for d in range(1, n):
+        pl.semaphore_signal(barrier, inc=1, device_id=to_peer(d), device_id_type=MESH)
+
+    @pl.when(jnp.logical_not(last))
+    def _():
+        pl.semaphore_signal(barrier, inc=1, device_id=down, device_id_type=MESH)
+
+    @pl.when(jnp.logical_not(first))
+    def _():
+        pl.semaphore_signal(barrier, inc=1, device_id=up, device_id_type=MESH)
+
+    inputs = [
+        pltpu.make_async_copy(src, dst, in_sem.at[j])
+        for j, (src, dst) in enumerate((
+            (w_hbm, w_in), (rates_hbm, rates), (m_hbm, m_in), (fw_hbm, fw_in), (fm_hbm, fm_in),
+        ))
+    ]
+    for copy in inputs:
+        copy.start()
+    loads = [[
+        pltpu.make_async_copy(src.at[b], dst.at[b], load_sem.at[j, b])
+        for b in range(total)
+    ] for j, (src, dst) in enumerate(((k_hbm, kbuf), (v_hbm, vbuf), (q_hbm, qbuf)))]
+    for b in range(total):
+        loads[0][b].start()
+        loads[1][b].start()
+    for b in range(total):
+        loads[2][b].start()
+
+    def fill_bank(e, source):
+        bank[e, outer, 0, inner] = source[0].astype(bf16)
+        bank[e, outer, 1, inner] = source[2].astype(bf16)
+        bank[e, 2, outer, inner] = source[1].astype(bf16)
+
+    def entry_copies(s):
+        e = total + s
+        pieces = (bank.at[e, outer, :, inner], bank.at[e, 2, outer, inner])
+        return [
+            rcopy(piece, piece, en_s.at[s, d, j], en_r.at[s, d, j], to_peer(d))
+            for j, piece in enumerate(pieces) for d in (1, 2, 3)
+        ]
+
+    def moment_copies(s):
+        return [
+            rcopy(mx.at[s], mr.at[s, tok], mx_s.at[s, d], mx_r.at[s, d], to_peer(d))
+            for d in (1, 2, 3)
+        ]
+
+    def square_copies():
+        return [rcopy(sq.at[tok], sq.at[tok], qs.at[d], qr.at[d], to_peer(d)) for d in (1, 2, 3)]
+
+    def start(copies):
+        for copy in copies:
+            copy.start()
+
+    def arrive(copies):
+        for copy in copies:
+            copy.wait_recv()
+
+    def take_state(s, weights, moments):
+        e = total + s
+        for item in range(3):
+            wst[item] = bank[e, item].astype(f32)
+        wst[outer, 0, inner] = weights[0]
+        wst[outer, 1, inner] = weights[2]
+        wst[2, outer, inner] = weights[1]
+        arrive(moment_copies(s))
+        for o in range(2):
+            for i in range(2):
+                @pl.when(tok != 2 * o + i)
+                def _():
+                    mst[o, 0, i] = mr[s, 2 * o + i, 0].astype(f32)
+                    mst[o, 1, i] = mr[s, 2 * o + i, 2].astype(f32)
+                    mst[2, o, i] = mr[s, 2 * o + i, 1].astype(f32)
+        mst[outer, 0, inner] = moments[0]
+        mst[outer, 1, inner] = moments[2]
+        mst[2, outer, inner] = moments[1]
+
+    inputs[0].wait()
+    fill_bank(total, w_in)
+    neighbours = (seg + segs - 1) // segs + (2 * segs - 2 - seg) // segs
+    pl.semaphore_wait(barrier, n - 1 + neighbours)
+    start(entry_copies(0))
+    inputs[1].wait()
+    for s in range(steps):
+        drawn = rates[s]
+        sums = jnp.sum(drawn * drawn, axis=1, keepdims=True)
+        sq[tok, s] = jnp.broadcast_to(sums, (blocks, LANES))
+    start(square_copies())
+    inputs[2].wait()
+    mx[0] = m_in[...].astype(bf16)
+    start(moment_copies(0))
+    inputs[3].wait()
+    inputs[4].wait()
+
+    def prepare_keys(b):
+        pltpu.make_async_copy(k_hbm.at[b], kbuf.at[b], load_sem.at[0, b]).wait()
+        kt[...] = kbuf[b].T
+
+    def prepare_values(b):
+        pltpu.make_async_copy(v_hbm.at[b], vbuf.at[b], load_sem.at[1, b]).wait()
+        s = b // blocks
+        row = jnp.broadcast_to(rates[s, pl.ds(b - s * blocks, 1), :], (LANES, rows))
+        column = jnp.concatenate([row.T] * (head // LANES), axis=1)
+        product = (column * vbuf[b].astype(f32)).astype(bf16)
+        scaled[...] = product
+        scaled_t[...] = product.T
+
+    def stage_copy(b, stage, item, p):
+        src = (gs, mid)[stage].at[b, item, p]
+        return rcopy(
+            src, got.at[b, stage, item, p],
+            st_s.at[b, stage, item, p], st_r.at[b, stage, item, p], stage_to[stage][p],
+        )
+
+    def relay_copy(b, s, item):
+        return rcopy(
+            bank.at[b, item], bank.at[total + s + 1, item],
+            rl_s.at[s, item], rl_r.at[s, item], down,
+        )
+
+    def m_copy(s, item):
+        return rcopy(msend.at[s, item], mrecv.at[s, item], mm_s.at[s, item], mm_r.at[s, item], down)
+
+    def matrix(slot, item):
+        return bank[slot, item].reshape(head, head)
+
+    def flow(b, slot, c):
+        w13 = matrix(slot, c)
+        w2 = matrix(slot, 2)[:, c * half:(c + 1) * half]
+
+        @pl.loop(0, tiles, unroll=UNROLL)
+        def _(i):
+            at = pl.ds(pl.multiple_of(i * tile, tile), tile)
+            both = mm_t(kbuf[b, at, :], w13)
+            back = mm(scaled[at, :], w2)
+            gate, up_pre = both[:, :half], both[:, half:]
+            sig = sigmoid(gate)
+            act = gate * sig
+            slope = sig + act * (1.0 - sig)
+            hid[at, c * half:(c + 1) * half] = (act * up_pre).astype(bf16)
+            bgu[c, at, :half] = (back * up_pre * slope).astype(bf16)
+            bgu[c, at, half:] = (back * act).astype(bf16)
+
+    def send_grads(b, item):
+        if item < 2:
+            grad = mm(kt[...], bgu[item]).T
+        else:
+            grad = mm(scaled_t[...], hid[...])
+        for p in range(2):
+            gs[b, item, p] = grad[p * half:(p + 1) * half].astype(bf16).reshape(gs.shape[3:])
+            stage_copy(b, 0, item, p).start()
+
+    def pair_sum(b, item):
+        for p in range(2):
+            stage_copy(b, 0, item, p).wait_recv()
+            mid[b, item, p] = (gs[b, item, p].astype(f32) + got[b, 0, item, p].astype(f32)).astype(bf16)
+            stage_copy(b, 1, item, p).start()
+
+    def update(b, item, factor):
+        for p in range(2):
+            stage_copy(b, 1, item, p).wait_recv()
+            grad = mid[b, item, p].astype(f32) + got[b, 1, item, p].astype(f32)
+            moment = momentum_decay * mst[item, p] - grad * factor
+            weight = wst[item, p]
+            stepped = weight - learn_rate * moment
+            before = jnp.sum(weight * weight, axis=2, keepdims=True)
+            after = jnp.sum(stepped * stepped, axis=2, keepdims=True)
+            weight = stepped * jnp.sqrt(before / (after + epsilon))
+            mst[item, p] = moment
+            wst[item, p] = weight
+            bank[b, item, p] = weight.astype(bf16)
+
+    def apply_fast(b, begin, stop):
+        if begin == 0:
+            pltpu.make_async_copy(q_hbm.at[b], qbuf.at[b], load_sem.at[2, b]).wait()
+        wa, wb, w2 = matrix(b, 0), matrix(b, 1), matrix(b, 2)
+
+        @pl.loop(begin, stop, unroll=min(UNROLL, stop - begin))
+        def _(i):
+            at = pl.ds(pl.multiple_of(i * tile, tile), tile)
+            asked = qbuf[b, at, :]
+            parts = []
+            for w13 in (wa, wb):
+                both = mm_t(asked, w13)
+                gate = both[:, :half]
+                parts.append((gate * sigmoid(gate) * both[:, half:]).astype(bf16))
+            obuf[b, at, :] = mm_t(jnp.concatenate(parts, axis=1), w2).astype(bf16)
+
+        if stop == tiles:
+            pltpu.make_async_copy(obuf.at[b], out_hbm.at[b], store_sem.at[b]).start()
+
+    prepare_keys(0)
+    prepare_values(0)
+    arrive(entry_copies(0))
+
+    @pl.when(first)
+    def _():
+        for s in range(1, steps):
+            fill_bank(total + s, fw_in)
+            mx[s] = fm_in[...].astype(bf16)
+            start(entry_copies(s))
+            start(moment_copies(s))
+
+    cut = (tiles + 1) // 2
+
+    @pl.loop(0, total)
+    def _(b):
+        s = b // blocks
+        g = b - s * blocks
+        inside = (g + blocks - 1) // blocks
+        slot = (total + s) * (1 - inside) + (b - 1) * inside
+        entered = jnp.logical_and(jnp.logical_and(g == 0, s > 0), jnp.logical_not(first))
+        renewed = jnp.logical_and(jnp.logical_and(g == 0, s > 0), first)
+        border = jnp.logical_and(g == blocks - 1, s < steps - 1)
+        passing = jnp.logical_and(border, jnp.logical_not(last))
+
+        @pl.when(renewed)
+        def _():
+            arrive(entry_copies(s))
+
+        @pl.when(entered)
+        def _():
+            for item in (0, 2):
+                relay_copy(b - 1, s - 1, item).wait_recv()
+
+        flow(b, slot, 0)
+        send_grads(b, 0)
+
+        @pl.when(entered)
+        def _():
+            relay_copy(b - 1, s - 1, 1).wait_recv()
+
+        flow(b, slot, 1)
+        send_grads(b, 2)
+        send_grads(b, 1)
+
+        @pl.when(jnp.logical_and(g == 0, s == 0))
+        def _():
+            arrive(square_copies())
+            take_state(0, w_in, m_in)
+
+        @pl.when(renewed)
+        def _():
+            take_state(s, fw_in, fm_in)
+
+        @pl.when(entered)
+        def _():
+            for item in range(3):
+                wst[item] = bank[total + s, item].astype(f32)
+
+        square = sq[0, s, pl.ds(g, 1), :]
+        for p in range(1, n):
+            square = square + sq[p, s, pl.ds(g, 1), :]
+        factor = lax.rsqrt(jnp.concatenate([square] * (head // LANES), axis=1))
+
+        @pl.when(g > 0)
+        def _():
+            apply_fast(b - 1, 0, cut)
+
+        @pl.when(b < total - 1)
+        def _():
+            prepare_keys(b + 1)
+
+        pair_sum(b, 0)
+
+        @pl.when(g > 0)
+        def _():
+            apply_fast(b - 1, cut, tiles)
+
+        pair_sum(b, 2)
+
+        @pl.when(b < total - 1)
+        def _():
+            prepare_values(b + 1)
+
+        pair_sum(b, 1)
+
+        @pl.when(entered)
+        def _():
+            for item in range(3):
+                m_copy(s - 1, item).wait_recv()
+                mst[item] = mrecv[s - 1, item].astype(f32)
+
+        for item in (0, 2, 1):
+            update(b, item, factor)
+
+            @pl.when(passing)
+            def _():
+                relay_copy(b, s, item).start()
+
+        @pl.when(passing)
+        def _():
+            for item in (0, 2, 1):
+                msend[s, item] = mst[item].astype(bf16)
+                m_copy(s, item).start()
+
+        @pl.when(g == blocks - 1)
+        def _():
+            apply_fast(b, 0, tiles)
+
+    for ref, state in ((w_out, wst), (m_out, mst)):
+        ref[0] = state[outer, 0, inner]
+        ref[2] = state[outer, 1, inner]
+        ref[1] = state[2, outer, inner]
+
+    def drain_entry(s):
+        for copy in entry_copies(s) + moment_copies(s):
+            copy.wait_send()
+
+    drain_entry(0)
+
+    @pl.when(first)
+    def _():
+        for s in range(1, steps):
+            drain_entry(s)
+
+    for copy in square_copies():
+        copy.wait_send()
+
+    @pl.when(jnp.logical_not(last))
+    def _():
+        for s in range(steps - 1):
+            for item in range(3):
+                relay_copy(s * blocks + blocks - 1, s, item).wait_send()
+                m_copy(s, item).wait_send()
+
+    @pl.loop(0, total)
+    def _(b):
+        for stage in range(2):
+            for item in range(3):
+                for p in range(2):
+                    stage_copy(b, stage, item, p).wait_send()
+        pltpu.make_async_copy(obuf.at[b], out_hbm.at[b], store_sem.at[b]).wait()
+
+
+def quad_scratch(steps, blocks, rows, head):
+    total = steps * blocks
+    quarter = head // 4
+    flat = (total, rows, head)
+    whole = (2, 2, quarter, head)
+    piece = (3, quarter, head)
+    dma = pltpu.SemaphoreType.DMA
+    vmem = pltpu.VMEM
+    return [vmem(flat, bf16)] * 4 + [
+        vmem((head, rows), bf16),
+        vmem((rows, head), bf16),
+        vmem((head, rows), bf16),
+        vmem((rows, head), bf16),
+        vmem((2, rows, head), bf16),
+        vmem((total + steps, 3) + whole, bf16),
+        vmem((total, 3) + whole, bf16),
+        vmem((total, 2, 3) + whole, bf16),
+        vmem((total, 3) + whole, bf16),
+        vmem((3,) + whole, f32),
+        vmem((3,) + whole, f32),
+        vmem(piece, f32),
+        vmem(piece, f32),
+        vmem(piece, f32),
+        vmem(piece, f32),
+        vmem((steps, blocks, rows), f32),
+        vmem((steps,) + piece, bf16),
+        vmem((steps, 4) + piece, bf16),
+        vmem((steps, 3) + whole, bf16),
+        vmem((steps, 3) + whole, bf16),
+        vmem((4, steps, blocks, LANES), f32),
+        dma((3, total)),
+        dma((total,)),
+        dma((5,)),
+        dma((total, 2, 3, 2)),
+        dma((total, 2, 3, 2)),
+        dma((steps, 4, 2)),
+        dma((steps, 4, 2)),
+        dma((steps, 3)),
+        dma((steps, 3)),
+        dma((steps, 3)),
+        dma((steps, 3)),
+        dma((steps, 4)),
+        dma((steps, 4)),
+        dma((4,)),
+        dma((4,)),
+    ]
+
+
 def body(n, segs, queries, keys, values, rates, weights, momenta, fresh_w, fresh_m):
     steps, _, blocks, rows, head = queries.shape
     total = steps * blocks
@@ -343,17 +763,13 @@
     dma = pltpu.SemaphoreType.DMA
     big = (rows, head)
     turned = (head, rows)
-    outs = pl.pallas_call(
-        functools.partial(kernel, n, segs, steps, blocks, tile),
-        out_shape=(
-            jax.ShapeDtypeStruct(flat, bf16),
-            jax.ShapeDtypeStruct(piece, f32),
-            jax.ShapeDtypeStruct(piece, f32),
-        ),
-        in_specs=[hbm, hbm, hbm, vmem, vmem, vmem, vmem, vmem],
-        out_specs=(hbm, vmem, vmem),
-        scratch_shapes=[pltpu.VMEM(flat, bf16)] * 4
-        + [
+    if n == 4 and head % 256 == 0:
+        run = functools.partial(quad_kernel, segs, steps, blocks, tile)
+        scratch = quad_scratch(steps, blocks, rows, head)
+        in_specs = [hbm] * 8
+    else:
+        run = functools.partial(kernel, n, segs, steps, blocks, tile)
+        scratch = [pltpu.VMEM(flat, bf16)] * 4 + [
             pltpu.VMEM(turned, bf16),
             pltpu.VMEM(big, bf16),
             pltpu.VMEM(turned, bf16),
@@ -378,7 +794,18 @@
             dma((steps,)),
             dma((n,)),
             dma((n,)),
-        ],
+        ]
+        in_specs = [hbm, hbm, hbm, vmem, vmem, vmem, vmem, vmem]
+    outs = pl.pallas_call(
+        run,
+        out_shape=(
+            jax.ShapeDtypeStruct(flat, bf16),
+            jax.ShapeDtypeStruct(piece, f32),
+            jax.ShapeDtypeStruct(piece, f32),
+        ),
+        in_specs=in_specs,
+        out_specs=(hbm, vmem, vmem),
+        scratch_shapes=scratch,
         compiler_params=pltpu.CompilerParams(
             collective_id=0, has_side_effects=True, vmem_limit_bytes=60 * 1024 * 1024
         ),

time: 70.1 us -> 73.1 us (1.043)
  Pallas kernels: 64.5 us -> 67.5 us
    pallas_call x1, Pallas kernels: 64.5 us -> 67.5 us  [body(): pl.pallas_call(run, out_shape=(jax.ShapeDtypeStruct(flat, bf16), jax.Shap...]
where the time goes in v2:
time: 73.1 us; the launch traced here: 72.9 us
  Pallas kernels  67.5 us (92%)
  local copies, waits for them, and re-layouts  4.81 us (7%)
    pallas_call x1, Pallas kernels, body(): pl.pallas_call(run, out_shape=(jax.ShapeDtypeStruct(flat, bf16), jax.Shap...  67.5 us
    unnamed x7, local copies, waits for them, and re-layouts  4.81 us

profile of v2, /device:TPU:0, one launch (start us, length us, event | category | flops | bytes accessed | tf_op | source)
XLA Modules:
  0.0 72.9 jit_solution(13443205306316297471)
XLA Ops:
  0.6 67.5 %shard_map.103 = (bf16[4,1280,256]{2,1,0:T(8,128)(2,1)}, f32[3,64,256]{2,1,0:T(8,128)}, f32[3,64,256]{2,1,0:T(8,128)}) custom-call(bf16[4,1280,256]{2,1,0:T(8,128)(2,1)} %bitcast.22, bf16[4,1280,256]{2,1,0:T(8,128)(2,1)} %bitcast.23, bf16[4,1280,256]{2,1,0:T(8,128)(2,1)} %bitcast.24, f32[2,2,1280]{2,1,0:T(2,128)} %bitcast.31, f32[3,64,256]{2,1,0:T(8,128)} %bitcast.27, ...), custom_call_target="tpu_custom_call" | custom-call | tf_op jit(solution)/shard_map/pallas_call | solution.py:799
  68.1 0.0 copy-start.1
  68.1 0.0 copy-start
  68.1 3.4 %copy.15 = bf16[2,1,2,1280,256]{4,3,2,1,0:T(8,128)(2,1)} copy(bf16[2,1,2,1280,256]{4,3,2,1,0:T(8,128)(2,1)} %bitcast.21) | data formatting | bytes 5242880
  71.6 0.0 copy-done.1
  71.6 0.7 copy.16
  72.3 0.0 copy-done
  72.3 0.7 copy.17
Async XLA Ops:
  68.1 3.5 %copy-start.1 = (f32[3,64,256]{2,1,0:T(8,128)S(1)}, f32[3,64,256]{2,1,0:T(8,128)}, u32[]{:S(2)}) copy-start(f32[3,64,256]{2,1,0:T(8,128)} %get-tuple-element.7) | copy-start | bytes 589828
  68.1 4.1 %copy-start = (f32[3,64,256]{2,1,0:T(8,128)S(1)}, f32[3,64,256]{2,1,0:T(8,128)}, u32[]{:S(2)}) copy-start(f32[3,64,256]{2,1,0:T(8,128)} %get-tuple-element.8) | copy-start | bytes 589828

commit v3 on v2

--- a/solution.py
+++ b/solution.py
@@ -336,7 +336,7 @@
     k_hbm, v_hbm, q_hbm, rates_hbm, w_hbm, m_hbm, fw_hbm, fm_hbm,
     out_hbm, w_out, m_out,
     kbuf, vbuf, qbuf, obuf, kt, scaled, scaled_t, hid, bgu,
-    bank, gs, got, mid, wst, mst,
+    bank, gs, got, mid, tot, wst, mst,
     w_in, m_in, fw_in, fm_in, rates, mx, mr, msend, mrecv, sq,
     load_sem, store_sem, in_sem, st_s, st_r, en_s, en_r, rl_s, rl_r, mm_s, mm_r, mx_s, mx_r, qs, qr,
 ):
@@ -356,7 +356,12 @@
     def to_peer(d):
         return {"seg": seg, "tok": peers[d]}
 
-    stage_to = ((to_peer(1), to_peer(2)), (to_peer(2), to_peer(1)))
+    gather_to = (to_peer(1), to_peer(2))
+    cross_to = (to_peer(2), to_peer(1))
+    own = (inner, outer)
+    far = (1 - inner, 1 - outer)
+    odd = lax.rem(seg, 2) == 1
+    even = jnp.logical_not(odd)
     down = {"seg": lax.rem(seg + 1, segs), "tok": tok}
     up = {"seg": lax.rem(seg + segs - 1, segs), "tok": tok}
 
@@ -381,20 +386,15 @@
     inputs = [
         pltpu.make_async_copy(src, dst, in_sem.at[j])
         for j, (src, dst) in enumerate((
-            (w_hbm, w_in), (rates_hbm, rates), (m_hbm, m_in), (fw_hbm, fw_in), (fm_hbm, fm_in),
+            (w_hbm, w_in), (m_hbm, m_in), (rates_hbm, rates), (fw_hbm, fw_in), (fm_hbm, fm_in),
         ))
     ]
-    for copy in inputs:
-        copy.start()
     loads = [[
         pltpu.make_async_copy(src.at[b], dst.at[b], load_sem.at[j, b])
         for b in range(total)
     ] for j, (src, dst) in enumerate(((k_hbm, kbuf), (v_hbm, vbuf), (q_hbm, qbuf)))]
-    for b in range(total):
-        loads[0][b].start()
-        loads[1][b].start()
-    for b in range(total):
-        loads[2][b].start()
+    for copy in (*inputs[:3], loads[0][0], loads[1][0]):
+        copy.start()
 
     def fill_bank(e, source):
         bank[e, outer, 0, inner] = source[0].astype(bf16)
@@ -426,13 +426,15 @@
         for copy in copies:
             copy.wait_recv()
 
-    def take_state(s, weights, moments):
+    def take_weights(s, weights):
         e = total + s
         for item in range(3):
             wst[item] = bank[e, item].astype(f32)
         wst[outer, 0, inner] = weights[0]
         wst[outer, 1, inner] = weights[2]
         wst[2, outer, inner] = weights[1]
+
+    def take_moments(s, moments):
         arrive(moment_copies(s))
         for o in range(2):
             for i in range(2):
@@ -450,17 +452,21 @@
     neighbours = (seg + segs - 1) // segs + (2 * segs - 2 - seg) // segs
     pl.semaphore_wait(barrier, n - 1 + neighbours)
     start(entry_copies(0))
+    for b in range(1, total):
+        loads[0][b].start()
+        loads[1][b].start()
+    for b in range(total):
+        loads[2][b].start()
+    for copy in inputs[3:]:
+        copy.start()
     inputs[1].wait()
+    mx[0] = m_in[...].astype(bf16)
+    inputs[2].wait()
     for s in range(steps):
         drawn = rates[s]
         sums = jnp.sum(drawn * drawn, axis=1, keepdims=True)
         sq[tok, s] = jnp.broadcast_to(sums, (blocks, LANES))
     start(square_copies())
-    inputs[2].wait()
-    mx[0] = m_in[...].astype(bf16)
-    start(moment_copies(0))
-    inputs[3].wait()
-    inputs[4].wait()
 
     def prepare_keys(b):
         pltpu.make_async_copy(k_hbm.at[b], kbuf.at[b], load_sem.at[0, b]).wait()
@@ -475,12 +481,21 @@
         scaled[...] = product
         scaled_t[...] = product.T
 
-    def stage_copy(b, stage, item, p):
-        src = (gs, mid)[stage].at[b, item, p]
+    def pair_copy(b, stage, item, p):
         return rcopy(
-            src, got.at[b, stage, item, p],
-            st_s.at[b, stage, item, p], st_r.at[b, stage, item, p], stage_to[stage][p],
+            (gs, mid)[stage].at[b, item, p], got.at[b, stage, item, p],
+            st_s.at[b, stage, item, p], st_r.at[b, stage, item, p], (gather_to, cross_to)[stage][p],
         )
+
+    def trio_copy(b, stage, item, p):
+        if stage == 0:
+            src, dst, peer = gs.at[b, item, p, far[p]], got.at[b, 0, item, p, 0], gather_to[p]
+        elif stage == 1:
+            src, dst, peer = mid.at[b, item, p, 0], got.at[b, 1, item, p, 0], cross_to[p]
+        else:
+            src, peer = tot.at[b, item, p, own[p]], gather_to[p]
+            dst = src
+        return rcopy(src, dst, st_s.at[b, stage, item, p], st_r.at[b, stage, item, p], peer)
 
     def relay_copy(b, s, item):
         return rcopy(
@@ -518,27 +533,66 @@
             grad = mm(scaled_t[...], hid[...])
         for p in range(2):
             gs[b, item, p] = grad[p * half:(p + 1) * half].astype(bf16).reshape(gs.shape[3:])
-            stage_copy(b, 0, item, p).start()
+
+            @pl.when(even)
+            def _():
+                pair_copy(b, 0, item, p).start()
+
+            @pl.when(odd)
+            def _():
+                trio_copy(b, 0, item, p).start()
 
     def pair_sum(b, item):
         for p in range(2):
-            stage_copy(b, 0, item, p).wait_recv()
+            pair_copy(b, 0, item, p).wait_recv()
             mid[b, item, p] = (gs[b, item, p].astype(f32) + got[b, 0, item, p].astype(f32)).astype(bf16)
-            stage_copy(b, 1, item, p).start()
-
-    def update(b, item, factor):
+            pair_copy(b, 1, item, p).start()
+
+    def trio_sum(b, item):
         for p in range(2):
-            stage_copy(b, 1, item, p).wait_recv()
-            grad = mid[b, item, p].astype(f32) + got[b, 1, item, p].astype(f32)
-            moment = momentum_decay * mst[item, p] - grad * factor
-            weight = wst[item, p]
-            stepped = weight - learn_rate * moment
-            before = jnp.sum(weight * weight, axis=2, keepdims=True)
-            after = jnp.sum(stepped * stepped, axis=2, keepdims=True)
-            weight = stepped * jnp.sqrt(before / (after + epsilon))
-            mst[item, p] = moment
-            wst[item, p] = weight
-            bank[b, item, p] = weight.astype(bf16)
+            trio_copy(b, 0, item, p).wait_recv()
+            mine = gs[b, item, p, own[p]].astype(f32)
+            mid[b, item, p, 0] = (mine + got[b, 0, item, p, 0].astype(f32)).astype(bf16)
+            trio_copy(b, 1, item, p).start()
+
+    def trio_cross(b, item):
+        for p in range(2):
+            trio_copy(b, 1, item, p).wait_recv()
+            both = mid[b, item, p, 0].astype(f32) + got[b, 1, item, p, 0].astype(f32)
+            tot[b, item, p, own[p]] = both.astype(bf16)
+            trio_copy(b, 2, item, p).start()
+
+    def step_half(b, item, p, factor, grad):
+        moment = momentum_decay * mst[item, p] - grad * factor
+        weight = wst[item, p]
+        stepped = weight - learn_rate * moment
+        before = jnp.sum(weight * weight, axis=2, keepdims=True)
+        after = jnp.sum(stepped * stepped, axis=2, keepdims=True)
+        weight = stepped * jnp.sqrt(before / (after + epsilon))
+        mst[item, p] = moment
+        wst[item, p] = weight
+        bank[b, item, p] = weight.astype(bf16)
+
+    def update(b, item):
+        s = b // blocks
+        g = b - s * blocks
+        square = sq[0, s, pl.ds(g, 1), :]
+        for p in range(1, n):
+            square = square + sq[p, s, pl.ds(g, 1), :]
+        factor = lax.rsqrt(jnp.concatenate([square] * (head // LANES), axis=1))
+
+        @pl.when(even)
+        def _():
+            for p in range(2):
+                pair_copy(b, 1, item, p).wait_recv()
+                grad = mid[b, item, p].astype(f32) + got[b, 1, item, p].astype(f32)
+                step_half(b, item, p, factor, grad)
+
+        @pl.when(odd)
+        def _():
+            for p in range(2):
+                trio_copy(b, 2, item, p).wait_recv()
+                step_half(b, item, p, factor, tot[b, item, p].astype(f32))
 
     def apply_fast(b, begin, stop):
         if begin == 0:
@@ -561,16 +615,12 @@
 
     prepare_keys(0)
     prepare_values(0)
+    for copy in entry_copies(0):
+        copy.wait_send()
+    start(moment_copies(0))
     arrive(entry_copies(0))
-
-    @pl.when(first)
-    def _():
-        for s in range(1, steps):
-            fill_bank(total + s, fw_in)
-            mx[s] = fm_in[...].astype(bf16)
-            start(entry_copies(s))
-            start(moment_copies(s))
-
+    for copy in inputs[3:]:
+        copy.wait()
     cut = (tiles + 1) // 2
 
     @pl.loop(0, total)
@@ -596,6 +646,10 @@
         flow(b, slot, 0)
         send_grads(b, 0)
 
+        @pl.when(g > 0)
+        def _():
+            update(b - 1, 1)
+
         @pl.when(entered)
         def _():
             relay_copy(b - 1, s - 1, 1).wait_recv()
@@ -604,69 +658,103 @@
         send_grads(b, 2)
         send_grads(b, 1)
 
-        @pl.when(jnp.logical_and(g == 0, s == 0))
+        @pl.when(b < total - 1)
+        def _():
+            prepare_keys(b + 1)
+
+        @pl.when(odd)
+        def _():
+            trio_sum(b, 0)
+
+        @pl.when(b > 0)
+        def _():
+            apply_fast(b - 1, 0, cut)
+
+        @pl.when(even)
+        def _():
+            pair_sum(b, 0)
+
+        @pl.when(odd)
+        def _():
+            trio_sum(b, 2)
+            trio_cross(b, 0)
+
+        @pl.when(b > 0)
+        def _():
+            apply_fast(b - 1, cut, tiles)
+
+        @pl.when(even)
+        def _():
+            pair_sum(b, 2)
+
+        @pl.when(odd)
+        def _():
+            trio_sum(b, 1)
+            trio_cross(b, 2)
+
+        @pl.when(b < total - 1)
+        def _():
+            prepare_values(b + 1)
+
+        @pl.when(even)
+        def _():
+            pair_sum(b, 1)
+
+        @pl.when(odd)
+        def _():
+            trio_cross(b, 1)
+
+        for step in range(1, steps):
+            @pl.when(jnp.logical_and(first, b == 0))
+            def _():
+                fill_bank(total + step, fw_in)
+                start(entry_copies(step))
+
+            @pl.when(jnp.logical_and(first, b == step * blocks - 1))
+            def _():
+                mx[step] = fm_in[...].astype(bf16)
+                start(moment_copies(step))
+
+        @pl.when(b == 0)
         def _():
             arrive(square_copies())
-            take_state(0, w_in, m_in)
+            take_weights(0, w_in)
+            take_moments(0, m_in)
 
         @pl.when(renewed)
         def _():
-            take_state(s, fw_in, fm_in)
+            take_weights(s, fw_in)
+            take_moments(s, fm_in)
 
         @pl.when(entered)
         def _():
             for item in range(3):
                 wst[item] = bank[total + s, item].astype(f32)
-
-        square = sq[0, s, pl.ds(g, 1), :]
-        for p in range(1, n):
-            square = square + sq[p, s, pl.ds(g, 1), :]
-        factor = lax.rsqrt(jnp.concatenate([square] * (head // LANES), axis=1))
-
-        @pl.when(g > 0)
-        def _():
-            apply_fast(b - 1, 0, cut)
-
-        @pl.when(b < total - 1)
-        def _():
-            prepare_keys(b + 1)
-
-        pair_sum(b, 0)
-
-        @pl.when(g > 0)
-        def _():
-            apply_fast(b - 1, cut, tiles)
-
-        pair_sum(b, 2)
-
-        @pl.when(b < total - 1)
-        def _():
-            prepare_values(b + 1)
-
-        pair_sum(b, 1)
-
-        @pl.when(entered)
-        def _():
             for item in range(3):
                 m_copy(s - 1, item).wait_recv()
                 mst[item] = mrecv[s - 1, item].astype(f32)
 
-        for item in (0, 2, 1):
-            update(b, item, factor)
+        def finish(item):
+            update(b, item)
 
             @pl.when(passing)
             def _():
                 relay_copy(b, s, item).start()
 
+        finish(0)
+        finish(2)
+
+        @pl.when(g == blocks - 1)
+        def _():
+            finish(1)
+
         @pl.when(passing)
         def _():
             for item in (0, 2, 1):
                 msend[s, item] = mst[item].astype(bf16)
                 m_copy(s, item).start()
 
-        @pl.when(g == blocks - 1)
-        def _():
-            apply_fast(b, 0, tiles)
+    apply_fast(total - 1, 0, tiles)
 
     for ref, state in ((w_out, wst), (m_out, mst)):
         ref[0] = state[outer, 0, inner]
@@ -677,7 +765,8 @@
         for copy in entry_copies(s) + moment_copies(s):
             copy.wait_send()
 
-    drain_entry(0)
+    for copy in moment_copies(0):
+        copy.wait_send()
 
     @pl.when(first)
     def _():
@@ -696,10 +785,20 @@
 
     @pl.loop(0, total)
     def _(b):
-        for stage in range(2):
-            for item in range(3):
-                for p in range(2):
-                    stage_copy(b, stage, item, p).wait_send()
+        @pl.when(even)
+        def _():
+            for stage in range(2):
+                for item in range(3):
+                    for p in range(2):
+                        pair_copy(b, stage, item, p).wait_send()
+
+        @pl.when(odd)
+        def _():
+            for stage in range(3):
+                for item in range(3):
+                    for p in range(2):
+                        trio_copy(b, stage, item, p).wait_send()
+
         pltpu.make_async_copy(obuf.at[b], out_hbm.at[b], store_sem.at[b]).wait()
 
 
@@ -721,6 +820,7 @@
         vmem((total, 3) + whole, bf16),
         vmem((total, 2, 3) + whole, bf16),
         vmem((total, 3) + whole, bf16),
+        vmem((total, 3) + whole, bf16),
         vmem((3,) + whole, f32),
         vmem((3,) + whole, f32),
         vmem(piece, f32),
@@ -736,8 +836,8 @@
         dma((3, total)),
         dma((total,)),
         dma((5,)),
-        dma((total, 2, 3, 2)),
-        dma((total, 2, 3, 2)),
+        dma((total, 3, 3, 2)),
+        dma((total, 3, 3, 2)),
         dma((steps, 4, 2)),
         dma((steps, 4, 2)),
         dma((steps, 3)),

time: 73.1 us -> 68 us (0.930)
  the two profiles are of different devices: /device:TPU:0 before, /device:TPU:1 now
where the time goes in v3:
time: 68 us; the launch traced here: 67.9 us
  Pallas kernels  62.4 us (92%)
  local copies, waits for them, and re-layouts  4.81 us (7%)
    pallas_call x1, Pallas kernels, body(): pl.pallas_call(run, out_shape=(jax.ShapeDtypeStruct(flat, bf16), jax.Shap...  62.4 us
    unnamed x7, local copies, waits for them, and re-layouts  4.81 us

profile of v3, /device:TPU:1, one launch (start us, length us, event | category | flops | bytes accessed | tf_op | source)
XLA Modules:
  0.0 67.9 jit_solution(15279017926987552918)
XLA Ops:
  0.6 62.4 %shard_map.103 = (bf16[4,1280,256]{2,1,0:T(8,128)(2,1)}, f32[3,64,256]{2,1,0:T(8,128)}, f32[3,64,256]{2,1,0:T(8,128)}) custom-call(bf16[4,1280,256]{2,1,0:T(8,128)(2,1)} %bitcast.22, bf16[4,1280,256]{2,1,0:T(8,128)(2,1)} %bitcast.23, bf16[4,1280,256]{2,1,0:T(8,128)(2,1)} %bitcast.24, f32[2,2,1280]{2,1,0:T(2,128)} %bitcast.31, f32[3,64,256]{2,1,0:T(8,128)} %bitcast.27, ...), custom_call_target="tpu_custom_call" | custom-call | tf_op jit(solution)/shard_map/pallas_call | solution.py:899
  63.0 0.0 copy-start.1
  63.0 0.0 copy-start
  63.0 3.4 %copy.15 = bf16[2,1,2,1280,256]{4,3,2,1,0:T(8,128)(2,1)} copy(bf16[2,1,2,1280,256]{4,3,2,1,0:T(8,128)(2,1)} %bitcast.21) | data formatting | bytes 5242880
  66.5 0.0 copy-done.1
  66.5 0.7 copy.16
  67.2 0.0 copy-done
  67.2 0.7 copy.17
Async XLA Ops:
  63.0 3.5 %copy-start.1 = (f32[3,64,256]{2,1,0:T(8,128)S(1)}, f32[3,64,256]{2,1,0:T(8,128)}, u32[]{:S(2)}) copy-start(f32[3,64,256]{2,1,0:T(8,128)} %get-tuple-element.7) | copy-start | bytes 589828
  63.0 4.1 %copy-start = (f32[3,64,256]{2,1,0:T(8,128)S(1)}, f32[3,64,256]{2,1,0:T(8,128)}, u32[]{:S(2)}) copy-start(f32[3,64,256]{2,1,0:T(8,128)} %get-tuple-element.8) | copy-start | bytes 589828

commit v4 on v3

--- a/solution.py
+++ b/solution.py
@@ -11,6 +11,7 @@
 epsilon = 1e-06
 LANES = 128
 UNROLL = 5
+QUAD_VMEM = 40 * 1024 * 1024
 MESH = pl.DeviceIdType.MESH
 f32 = jnp.float32
 bf16 = jnp.bfloat16
@@ -331,14 +332,29 @@
         pltpu.make_async_copy(obuf.at[b], out_hbm.at[b], store_sem.at[b]).wait()
 
 
+def apply_tiles(begin, stop, tile, weights, asked_ref, out_ref):
+    half = asked_ref.shape[-1] // 2
+
+    @pl.loop(begin, stop, unroll=min(UNROLL, stop - begin))
+    def _(i):
+        at = pl.ds(pl.multiple_of(i * tile, tile), tile)
+        asked = asked_ref[at, :]
+        parts = []
+        for w13 in weights[:2]:
+            both = mm_t(asked, w13)
+            gate = both[:, :half]
+            parts.append((gate * sigmoid(gate) * both[:, half:]).astype(bf16))
+        out_ref[at, :] = mm_t(jnp.concatenate(parts, axis=1), weights[2]).astype(bf16)
+
+
 def quad_kernel(
     segs, steps, blocks, tile,
     k_hbm, v_hbm, q_hbm, rates_hbm, w_hbm, m_hbm, fw_hbm, fm_hbm,
-    out_hbm, w_out, m_out,
-    kbuf, vbuf, qbuf, obuf, kt, scaled, scaled_t, hid, bgu,
+    obuf, usable, asked_last, w_out, m_out,
+    kbuf, vbuf, qbuf, kt, scaled, scaled_t, hid, bgu,
     bank, gs, got, mid, tot, wst, mst,
     w_in, m_in, fw_in, fm_in, rates, mx, mr, msend, mrecv, sq,
-    load_sem, store_sem, in_sem, st_s, st_r, en_s, en_r, rl_s, rl_r, mm_s, mm_r, mx_s, mx_r, qs, qr,
+    load_sem, in_sem, st_s, st_r, en_s, en_r, rl_s, rl_r, mm_s, mm_r, mx_s, mx_r, qs, qr,
 ):
     total = steps * blocks
     n = 4
@@ -391,8 +407,9 @@
     ]
     loads = [[
         pltpu.make_async_copy(src.at[b], dst.at[b], load_sem.at[j, b])
-        for b in range(total)
+        for b in range(total - (j == 2))
     ] for j, (src, dst) in enumerate(((k_hbm, kbuf), (v_hbm, vbuf), (q_hbm, qbuf)))]
+    late = pltpu.make_async_copy(q_hbm.at[total - 1], asked_last, load_sem.at[2, total - 1])
     for copy in (*inputs[:3], loads[0][0], loads[1][0]):
         copy.start()
 
@@ -455,8 +472,9 @@
     for b in range(1, total):
         loads[0][b].start()
         loads[1][b].start()
-    for b in range(total):
-        loads[2][b].start()
+    for copy in loads[2]:
+        copy.start()
+    late.start()
     for copy in inputs[3:]:
         copy.start()
     inputs[1].wait()
@@ -597,21 +615,7 @@
     def apply_fast(b, begin, stop):
         if begin == 0:
             pltpu.make_async_copy(q_hbm.at[b], qbuf.at[b], load_sem.at[2, b]).wait()
-        wa, wb, w2 = matrix(b, 0), matrix(b, 1), matrix(b, 2)
-
-        @pl.loop(begin, stop, unroll=min(UNROLL, stop - begin))
-        def _(i):
-            at = pl.ds(pl.multiple_of(i * tile, tile), tile)
-            asked = qbuf[b, at, :]
-            parts = []
-            for w13 in (wa, wb):
-                both = mm_t(asked, w13)
-                gate = both[:, :half]
-                parts.append((gate * sigmoid(gate) * both[:, half:]).astype(bf16))
-            obuf[b, at, :] = mm_t(jnp.concatenate(parts, axis=1), w2).astype(bf16)
-
-        if stop == tiles:
-            pltpu.make_async_copy(obuf.at[b], out_hbm.at[b], store_sem.at[b]).start()
+        apply_tiles(begin, stop, tile, [matrix(b, item) for item in range(3)], qbuf.at[b], obuf.at[b])
 
     prepare_keys(0)
     prepare_values(0)
@@ -754,8 +758,8 @@
                 msend[s, item] = mst[item].astype(bf16)
                 m_copy(s, item).start()
 
-    apply_fast(total - 1, 0, tiles)
-
+    usable[...] = bank[total - 1]
+    late.wait()
     for ref, state in ((w_out, wst), (m_out, mst)):
         ref[0] = state[outer, 0, inner]
         ref[2] = state[outer, 1, inner]
@@ -799,7 +803,29 @@
                     for p in range(2):
                         trio_copy(b, stage, item, p).wait_send()
 
-        pltpu.make_async_copy(obuf.at[b], out_hbm.at[b], store_sem.at[b]).wait()
+
+def tail_kernel(
+    tile, done, usable, asked, w_ready, m_ready, out_hbm, w_hbm, m_hbm, obuf, sem,
+):
+    count = done.shape[0]
+    rows, head = asked.shape
+    copies = [
+        pltpu.make_async_copy(src, dst, sem.at[j])
+        for j, (src, dst) in enumerate(
+            [(w_ready, w_hbm), (m_ready, m_hbm)] + [(done.at[b], out_hbm.at[b]) for b in range(count)]
+        )
+    ]
+    for copy in copies:
+        copy.start()
+    weights = [usable[item].reshape(head, head) for item in range(3)]
+    for i in range(rows // tile):
+        apply_tiles(i, i + 1, tile, weights, asked, obuf)
+        at = pl.ds(i * tile, tile)
+        copy = pltpu.make_async_copy(obuf.at[at], out_hbm.at[count, at], sem.at[count + 2 + i])
+        copy.start()
+        copies.append(copy)
+    for copy in copies:
+        copy.wait()
 
 
 def quad_scratch(steps, blocks, rows, head):
@@ -810,7 +836,8 @@
     piece = (3, quarter, head)
     dma = pltpu.SemaphoreType.DMA
     vmem = pltpu.VMEM
-    return [vmem(flat, bf16)] * 4 + [
+    return [vmem(flat, bf16)] * 2 + [
+        vmem((total - 1, rows, head), bf16),
         vmem((head, rows), bf16),
         vmem((rows, head), bf16),
         vmem((head, rows), bf16),
@@ -834,7 +861,6 @@
         vmem((steps, 3) + whole, bf16),
         vmem((4, steps, blocks, LANES), f32),
         dma((3, total)),
-        dma((total,)),
         dma((5,)),
         dma((total, 3, 3, 2)),
         dma((total, 3, 3, 2)),
@@ -863,57 +889,76 @@
     dma = pltpu.SemaphoreType.DMA
     big = (rows, head)
     turned = (head, rows)
-    if n == 4 and head % 256 == 0:
-        run = functools.partial(quad_kernel, segs, steps, blocks, tile)
-        scratch = quad_scratch(steps, blocks, rows, head)
-        in_specs = [hbm] * 8
-    else:
-        run = functools.partial(kernel, n, segs, steps, blocks, tile)
-        scratch = [pltpu.VMEM(flat, bf16)] * 4 + [
-            pltpu.VMEM(turned, bf16),
-            pltpu.VMEM(big, bf16),
-            pltpu.VMEM(turned, bf16),
-            pltpu.VMEM(big, bf16),
-            pltpu.VMEM(big, bf16),
-            pltpu.VMEM(big, bf16),
-            pltpu.VMEM((3, head, head), bf16),
-            pltpu.VMEM((total, n) + piece, bf16),
-            pltpu.VMEM((total + steps, 3, head, head), bf16),
-            pltpu.VMEM((steps,) + piece, bf16),
-            pltpu.VMEM((steps,) + piece, bf16),
-            pltpu.VMEM((n, steps, blocks, LANES), f32),
-            dma((3, total)),
-            dma((total,)),
-            dma((total, n, 3)),
-            dma((total, n, 3)),
-            dma((total, n, 3)),
-            dma((total, n, 3)),
-            dma((steps, n, 3)),
-            dma((steps, n, 3)),
-            dma((steps,)),
-            dma((steps,)),
-            dma((n,)),
-            dma((n,)),
-        ]
-        in_specs = [hbm, hbm, hbm, vmem, vmem, vmem, vmem, vmem]
-    outs = pl.pallas_call(
-        run,
-        out_shape=(
-            jax.ShapeDtypeStruct(flat, bf16),
-            jax.ShapeDtypeStruct(piece, f32),
-            jax.ShapeDtypeStruct(piece, f32),
-        ),
-        in_specs=in_specs,
-        out_specs=(hbm, vmem, vmem),
-        scratch_shapes=scratch,
-        compiler_params=pltpu.CompilerParams(
-            collective_id=0, has_side_effects=True, vmem_limit_bytes=60 * 1024 * 1024
-        ),
-    )(
+    operands = (
         keys.reshape(flat), values.reshape(flat), queries.reshape(flat), rates[:, 0],
         jnp.swapaxes(weights[0], 1, 2), jnp.swapaxes(momenta[0], 1, 2),
         jnp.swapaxes(fresh_w, 1, 2), jnp.swapaxes(fresh_m, 1, 2),
     )
+    results = (
+        jax.ShapeDtypeStruct(flat, bf16),
+        jax.ShapeDtypeStruct(piece, f32),
+        jax.ShapeDtypeStruct(piece, f32),
+    )
+    if n == 4 and head % 256 == 0:
+        ready = pl.pallas_call(
+            functools.partial(quad_kernel, segs, steps, blocks, tile),
+            out_shape=(
+                jax.ShapeDtypeStruct((total - 1, rows, head), bf16),
+                jax.ShapeDtypeStruct((3, 2, 2, head // 4, head), bf16),
+                jax.ShapeDtypeStruct(big, bf16),
+                *results[1:],
+            ),
+            in_specs=[pl.BlockSpec(memory_space=pltpu.HBM)] * 8,
+            out_specs=(vmem,) * 5,
+            scratch_shapes=quad_scratch(steps, blocks, rows, head),
+            compiler_params=pltpu.CompilerParams(
+                collective_id=0, has_side_effects=True, vmem_limit_bytes=QUAD_VMEM
+            ),
+        )(*(pltpu.with_memory_space_constraint(x, pltpu.HBM) for x in operands))
+        outs = pl.pallas_call(
+            functools.partial(tail_kernel, tile),
+            out_shape=results,
+            in_specs=[vmem] * 5,
+            out_specs=(hbm,) * 3,
+            scratch_shapes=[pltpu.VMEM(big, bf16), dma((total + 1 + rows // tile,))],
+            compiler_params=pltpu.CompilerParams(vmem_limit_bytes=16 * 1024 * 1024),
+        )(*ready)
+    else:
+        outs = pl.pallas_call(
+            functools.partial(kernel, n, segs, steps, blocks, tile),
+            out_shape=results,
+            in_specs=[hbm, hbm, hbm, vmem, vmem, vmem, vmem, vmem],
+            out_specs=(hbm, vmem, vmem),
+            scratch_shapes=[pltpu.VMEM(flat, bf16)] * 4 + [
+                pltpu.VMEM(turned, bf16),
+                pltpu.VMEM(big, bf16),
+                pltpu.VMEM(turned, bf16),
+                pltpu.VMEM(big, bf16),
+                pltpu.VMEM(big, bf16),
+                pltpu.VMEM(big, bf16),
+                pltpu.VMEM((3, head, head), bf16),
+                pltpu.VMEM((total, n) + piece, bf16),
+                pltpu.VMEM((total + steps, 3, head, head), bf16),
+                pltpu.VMEM((steps,) + piece, bf16),
+                pltpu.VMEM((steps,) + piece, bf16),
+                pltpu.VMEM((n, steps, blocks, LANES), f32),
+                dma((3, total)),
+                dma((total,)),
+                dma((total, n, 3)),
+                dma((total, n, 3)),
+                dma((total, n, 3)),
+                dma((total, n, 3)),
+                dma((steps, n, 3)),
+                dma((steps, n, 3)),
+                dma((steps,)),
+                dma((steps,)),
+                dma((n,)),
+                dma((n,)),
+        ],
+            compiler_params=pltpu.CompilerParams(
+                collective_id=0, has_side_effects=True, vmem_limit_bytes=60 * 1024 * 1024
+            ),
+        )(*operands)
     return (
         outs[0].reshape(queries.shape),
         jnp.swapaxes(outs[1], 1, 2)[None],

time: 68 us -> 62.6 us (0.921)
  local copies, waits for them, and re-layouts: 4.81 us -> 0 us
    unnamed x7 -> x0, local copies, waits for them, and re-layouts: 4.81 us -> none
    pallas_call x1 -> x2, Pallas kernels: 62.4 us -> 61.8 us  [the longest x1 59.8 us: body(): pl.pallas_call(functools.partial(quad_kernel, segs, steps, blocks, tile),...]
where the time goes in v4:
time: 62.6 us; the launch traced here: 62.4 us
  Pallas kernels  61.8 us (99%)
  between operations  0.64 us (1%)
    pallas_call x1, Pallas kernels, body(): pl.pallas_call(functools.partial(quad_kernel, segs, steps, blocks, tile),...  59.8 us
    pallas_call x1, Pallas kernels, body(): pl.pallas_call(functools.partial(tail_kernel, tile), out_shape=results, i...  1.98 us

profile of v4, /device:TPU:1, one launch (start us, length us, event | category | flops | bytes accessed | tf_op | source)
XLA Modules:
  0.0 62.4 jit_solution(18170345865457826220)
XLA Ops:
  0.6 59.8 %shard_map.103 = (bf16[3,1280,256]{2,1,0:T(8,128)(2,1)S(1)}, bf16[3,2,2,64,256]{4,3,2,1,0:T(8,128)(2,1)S(1)}, bf16[1280,256]{1,0:T(8,128)(2,1)S(1)}, f32[3,64,256]{2,1,0:T(8,128)S(1)}, f32[3,64,256]{2,1,0:T(8,128)S(1)}) custom-call(bf16[4,1280,256]{2,1,0:T(8,128)(2,1)} %bitcast.21, bf16[4,1280,256]{2,1,0:T(8,128)(2,1)} %bitcast.22, ...), custom_call_target="tpu_custom_call" | custom-call | tf_op jit(solution)/shard_map/pallas_call | solution.py:903
  60.4 2.0 %shard_map.104 = (bf16[4,1280,256]{2,1,0:T(8,128)(2,1)}, f32[3,64,256]{2,1,0:T(8,128)}, f32[3,64,256]{2,1,0:T(8,128)}) custom-call(bf16[3,1280,256]{2,1,0:T(8,128)(2,1)S(1)} %get-tuple-element.11.done, bf16[3,2,2,64,256]{4,3,2,1,0:T(8,128)(2,1)S(1)} %get-tuple-element.12.usable, bf16[1280,256]{1,0:T(8,128)(2,1)S(1)} %get-tuple-element.13.asked, ...), custom_call_target="tpu_custom_call" | custom-call | tf_op jit(solution)/shard_map/pallas_call | solution.py:918

commit v5 on v4

--- a/solution.py
+++ b/solution.py
@@ -405,12 +405,18 @@
             (w_hbm, w_in), (m_hbm, m_in), (rates_hbm, rates), (fw_hbm, fw_in), (fm_hbm, fm_in),
         ))
     ]
-    loads = [[
-        pltpu.make_async_copy(src.at[b], dst.at[b], load_sem.at[j, b])
-        for b in range(total - (j == 2))
-    ] for j, (src, dst) in enumerate(((k_hbm, kbuf), (v_hbm, vbuf), (q_hbm, qbuf)))]
-    late = pltpu.make_async_copy(q_hbm.at[total - 1], asked_last, load_sem.at[2, total - 1])
-    for copy in (*inputs[:3], loads[0][0], loads[1][0]):
+    early = [
+        pltpu.make_async_copy(src.at[0], dst.at[0], load_sem.at[j])
+        for j, (src, dst) in enumerate(((k_hbm, kbuf), (v_hbm, vbuf)))
+    ]
+    rest = pl.ds(1, total - 1)
+    later = [
+        pltpu.make_async_copy(k_hbm.at[rest], kbuf.at[rest], load_sem.at[2]),
+        pltpu.make_async_copy(v_hbm.at[rest], vbuf.at[rest], load_sem.at[3]),
+        pltpu.make_async_copy(q_hbm.at[pl.ds(0, total - 1)], qbuf, load_sem.at[4]),
+        pltpu.make_async_copy(q_hbm.at[total - 1], asked_last, load_sem.at[5]),
+    ]
+    for copy in (*inputs[:3], *early):
         copy.start()
 
     def fill_bank(e, source):
@@ -418,22 +424,44 @@
         bank[e, outer, 1, inner] = source[2].astype(bf16)
         bank[e, 2, outer, inner] = source[1].astype(bf16)
 
-    def entry_copies(s):
+    def entry_copy(s, j, d):
         e = total + s
-        pieces = (bank.at[e, outer, :, inner], bank.at[e, 2, outer, inner])
-        return [
-            rcopy(piece, piece, en_s.at[s, d, j], en_r.at[s, d, j], to_peer(d))
-            for j, piece in enumerate(pieces) for d in (1, 2, 3)
-        ]
+        piece = bank.at[e, 2, outer, inner] if j else bank.at[e, outer, :, inner]
+        return rcopy(piece, piece, en_s.at[d - 1, j], en_r.at[s, d - 1, j], to_peer(d))
+
+    def start_entry(s):
+        @pl.when(outer == 0)
+        def _():
+            for j in (0, 1):
+                for d in (3, 1, 2):
+                    entry_copy(s, j, d).start()
+
+        @pl.when(outer == 1)
+        def _():
+            for j in (1, 0):
+                for d in (3, 1, 2):
+                    entry_copy(s, j, d).start()
+
+    def arrive_entry(s, c):
+        @pl.when(outer == c)
+        def _():
+            entry_copy(s, 0, 1).wait_recv()
+
+        @pl.when(outer != c)
+        def _():
+            for d in (2, 3):
+                entry_copy(s, 0, d).wait_recv()
 
     def moment_copies(s):
         return [
-            rcopy(mx.at[s], mr.at[s, tok], mx_s.at[s, d], mx_r.at[s, d], to_peer(d))
+            rcopy(mx.at[s], mr.at[s, tok], mx_s.at[d - 1], mx_r.at[s, d - 1], to_peer(d))
             for d in (1, 2, 3)
         ]
 
     def square_copies():
-        return [rcopy(sq.at[tok], sq.at[tok], qs.at[d], qr.at[d], to_peer(d)) for d in (1, 2, 3)]
+        return [
+            rcopy(sq.at[tok], sq.at[tok], qs.at[d - 1], qr.at[d - 1], to_peer(d)) for d in (1, 2, 3)
+        ]
 
     def start(copies):
         for copy in copies:
@@ -468,13 +496,9 @@
     fill_bank(total, w_in)
     neighbours = (seg + segs - 1) // segs + (2 * segs - 2 - seg) // segs
     pl.semaphore_wait(barrier, n - 1 + neighbours)
-    start(entry_copies(0))
-    for b in range(1, total):
-        loads[0][b].start()
-        loads[1][b].start()
-    for copy in loads[2]:
+    start_entry(0)
+    for copy in later:
         copy.start()
-    late.start()
     for copy in inputs[3:]:
         copy.start()
     inputs[1].wait()
@@ -487,11 +511,9 @@
     start(square_copies())
 
     def prepare_keys(b):
-        pltpu.make_async_copy(k_hbm.at[b], kbuf.at[b], load_sem.at[0, b]).wait()
         kt[...] = kbuf[b].T
 
     def prepare_values(b):
-        pltpu.make_async_copy(v_hbm.at[b], vbuf.at[b], load_sem.at[1, b]).wait()
         s = b // blocks
         row = jnp.broadcast_to(rates[s, pl.ds(b - s * blocks, 1), :], (LANES, rows))
         column = jnp.concatenate([row.T] * (head // LANES), axis=1)
@@ -502,7 +524,7 @@
     def pair_copy(b, stage, item, p):
         return rcopy(
             (gs, mid)[stage].at[b, item, p], got.at[b, stage, item, p],
-            st_s.at[b, stage, item, p], st_r.at[b, stage, item, p], (gather_to, cross_to)[stage][p],
+            st_s.at[item, p], st_r.at[lax.rem(b, 2), stage, item, p], (gather_to, cross_to)[stage][p],
         )
 
     def trio_copy(b, stage, item, p):
@@ -513,7 +535,7 @@
         else:
             src, peer = tot.at[b, item, p, own[p]], gather_to[p]
             dst = src
-        return rcopy(src, dst, st_s.at[b, stage, item, p], st_r.at[b, stage, item, p], peer)
+        return rcopy(src, dst, st_s.at[item, p], st_r.at[lax.rem(b, 2), stage, item, p], peer)
 
     def relay_copy(b, s, item):
         return rcopy(
@@ -546,11 +568,19 @@
 
     def send_grads(b, item):
         if item < 2:
-            grad = mm(kt[...], bgu[item]).T
+            grad = mm(kt[...], bgu[item]).astype(bf16).T
         else:
-            grad = mm(scaled_t[...], hid[...])
+            grad = mm(scaled_t[...], hid[...]).astype(bf16)
         for p in range(2):
-            gs[b, item, p] = grad[p * half:(p + 1) * half].astype(bf16).reshape(gs.shape[3:])
+            gs[b, item, p] = grad[p * half:(p + 1) * half].reshape(gs.shape[3:])
+
+            @pl.when(jnp.logical_and(even, b > 0))
+            def _():
+                pair_copy(b - 1, 1, item, p).wait_send()
+
+            @pl.when(jnp.logical_and(odd, b > 0))
+            def _():
+                trio_copy(b - 1, 2, item, p).wait_send()
 
             @pl.when(even)
             def _():
@@ -564,6 +594,7 @@
         for p in range(2):
             pair_copy(b, 0, item, p).wait_recv()
             mid[b, item, p] = (gs[b, item, p].astype(f32) + got[b, 0, item, p].astype(f32)).astype(bf16)
+            pair_copy(b, 0, item, p).wait_send()
             pair_copy(b, 1, item, p).start()
 
     def trio_sum(b, item):
@@ -571,6 +602,7 @@
             trio_copy(b, 0, item, p).wait_recv()
             mine = gs[b, item, p, own[p]].astype(f32)
             mid[b, item, p, 0] = (mine + got[b, 0, item, p, 0].astype(f32)).astype(bf16)
+            trio_copy(b, 0, item, p).wait_send()
             trio_copy(b, 1, item, p).start()
 
     def trio_cross(b, item):
@@ -578,6 +610,7 @@
             trio_copy(b, 1, item, p).wait_recv()
             both = mid[b, item, p, 0].astype(f32) + got[b, 1, item, p, 0].astype(f32)
             tot[b, item, p, own[p]] = both.astype(bf16)
+            trio_copy(b, 1, item, p).wait_send()
             trio_copy(b, 2, item, p).start()
 
     def step_half(b, item, p, factor, grad):
@@ -613,16 +646,15 @@
                 step_half(b, item, p, factor, tot[b, item, p].astype(f32))
 
     def apply_fast(b, begin, stop):
-        if begin == 0:
-            pltpu.make_async_copy(q_hbm.at[b], qbuf.at[b], load_sem.at[2, b]).wait()
         apply_tiles(begin, stop, tile, [matrix(b, item) for item in range(3)], qbuf.at[b], obuf.at[b])
 
+    early[0].wait()
     prepare_keys(0)
+    early[1].wait()
     prepare_values(0)
-    for copy in entry_copies(0):
-        copy.wait_send()
+    for j in range(2):
+        entry_copy(0, j, 3).wait_send()
     start(moment_copies(0))
-    arrive(entry_copies(0))
     for copy in inputs[3:]:
         copy.wait()
     cut = (tiles + 1) // 2
@@ -638,9 +670,13 @@
         border = jnp.logical_and(g == blocks - 1, s < steps - 1)
         passing = jnp.logical_and(border, jnp.logical_not(last))
 
-        @pl.when(renewed)
-        def _():
-            arrive(entry_copies(s))
+        newly = jnp.logical_and(g == 0, jnp.logical_or(first, s == 0))
+
+        @pl.when(newly)
+        def _():
+            for d in (1, 2, 3):
+                entry_copy(s, 1, d).wait_recv()
+            arrive_entry(s, 0)
 
         @pl.when(entered)
         def _():
@@ -653,6 +689,10 @@
         @pl.when(g > 0)
         def _():
             update(b - 1, 1)
+
+        @pl.when(newly)
+        def _():
+            arrive_entry(s, 1)
 
         @pl.when(entered)
         def _():
@@ -662,6 +702,11 @@
         send_grads(b, 2)
         send_grads(b, 1)
 
+        @pl.when(b == 0)
+        def _():
+            for copy in later[:3]:
+                copy.wait()
+
         @pl.when(b < total - 1)
         def _():
             prepare_keys(b + 1)
@@ -703,19 +748,20 @@
         @pl.when(even)
         def _():
             pair_sum(b, 1)
-
-        @pl.when(odd)
-        def _():
-            trio_cross(b, 1)
 
         for step in range(1, steps):
             @pl.when(jnp.logical_and(first, b == 0))
             def _():
                 fill_bank(total + step, fw_in)
-                start(entry_copies(step))
+                for j in range(2):
+                    for d in (1, 2) if step == 1 else (1, 2, 3):
+                        entry_copy(step - 1, j, d).wait_send()
+                start_entry(step)
 
             @pl.when(jnp.logical_and(first, b == step * blocks - 1))
             def _():
+                for copy in moment_copies(step - 1):
+                    copy.wait_send()
                 mx[step] = fm_in[...].astype(bf16)
                 start(moment_copies(step))
 
@@ -746,6 +792,11 @@
                 relay_copy(b, s, item).start()
 
         finish(0)
+
+        @pl.when(odd)
+        def _():
+            trio_cross(b, 1)
+
         finish(2)
 
         @pl.when(g == blocks - 1)
@@ -759,23 +810,29 @@
                 m_copy(s, item).start()
 
     usable[...] = bank[total - 1]
-    late.wait()
+    later[3].wait()
     for ref, state in ((w_out, wst), (m_out, mst)):
         ref[0] = state[outer, 0, inner]
         ref[2] = state[outer, 1, inner]
         ref[1] = state[2, outer, inner]
 
-    def drain_entry(s):
-        for copy in entry_copies(s) + moment_copies(s):
+    def drain_entry(peers_left):
+        for j in range(2):
+            for d in peers_left:
+                entry_copy(0, j, d).wait_send()
+        for copy in moment_copies(0):
             copy.wait_send()
 
-    for copy in moment_copies(0):
-        copy.wait_send()
-
-    @pl.when(first)
-    def _():
-        for s in range(1, steps):
-            drain_entry(s)
+    if steps > 1:
+        @pl.when(first)
+        def _():
+            drain_entry((1, 2, 3))
+
+        @pl.when(jnp.logical_not(first))
+        def _():
+            drain_entry((1, 2))
+    else:
+        drain_entry((1, 2))
 
     for copy in square_copies():
         copy.wait_send()
@@ -787,21 +844,15 @@
                 relay_copy(s * blocks + blocks - 1, s, item).wait_send()
                 m_copy(s, item).wait_send()
 
-    @pl.loop(0, total)
-    def _(b):
-        @pl.when(even)
-        def _():
-            for stage in range(2):
-                for item in range(3):
-                    for p in range(2):
-                        pair_copy(b, stage, item, p).wait_send()
-
-        @pl.when(odd)
-        def _():
-            for stage in range(3):
-                for item in range(3):
-                    for p in range(2):
-                        trio_copy(b, stage, item, p).wait_send()
+    for item in range(3):
+        for p in range(2):
+            @pl.when(even)
+            def _():
+                pair_copy(total - 1, 1, item, p).wait_send()
+
+            @pl.when(odd)
+            def _():
+                trio_copy(total - 1, 2, item, p).wait_send()
 
 
 def tail_kernel(
@@ -860,20 +911,20 @@
         vmem((steps, 3) + whole, bf16),
         vmem((steps, 3) + whole, bf16),
         vmem((4, steps, blocks, LANES), f32),
-        dma((3, total)),
+        dma((6,)),
         dma((5,)),
-        dma((total, 3, 3, 2)),
-        dma((total, 3, 3, 2)),
-        dma((steps, 4, 2)),
-        dma((steps, 4, 2)),
+        dma((3, 2)),
+        dma((2, 3, 3, 2)),
+        dma((3, 2)),
+        dma((steps, 3, 2)),
+        dma((steps - 1, 3)),
+        dma((steps - 1, 3)),
+        dma((steps - 1, 3)),
+        dma((steps - 1, 3)),
+        dma((3,)),
         dma((steps, 3)),
-        dma((steps, 3)),
-        dma((steps, 3)),
-        dma((steps, 3)),
-        dma((steps, 4)),
-        dma((steps, 4)),
-        dma((4,)),
-        dma((4,)),
+        dma((3,)),
+        dma((3,)),
     ]
 
 
@@ -899,7 +950,7 @@
         jax.ShapeDtypeStruct(piece, f32),
         jax.ShapeDtypeStruct(piece, f32),
     )
-    if n == 4 and head % 256 == 0:
+    if n == 4 and head % 256 == 0 and min(steps, blocks) > 1:
         ready = pl.pallas_call(
             functools.partial(quad_kernel, segs, steps, blocks, tile),
             out_shape=(

time: 62.6 us -> 60.8 us (0.971)
  Pallas kernels: 61.8 us -> 60 us
    pallas_call x1, Pallas kernels: 59.8 us -> 58.1 us  [body(): pl.pallas_call(functools.partial(quad_kernel, segs, steps, blocks, tile),...]
where the time goes in v5:
time: 60.8 us; the launch traced here: 60.7 us
  Pallas kernels  60 us (99%)
  between operations  0.64 us (1%)
    pallas_call x1, Pallas kernels, body(): pl.pallas_call(functools.partial(quad_kernel, segs, steps, blocks, tile),...  58.1 us
    pallas_call x1, Pallas kernels, body(): pl.pallas_call(functools.partial(tail_kernel, tile), out_shape=results, i...  1.98 us

profile of v5, /device:TPU:1, one launch (start us, length us, event | category | flops | bytes accessed | tf_op | source)
XLA Modules:
  0.0 60.7 jit_solution(4159422555735730588)
XLA Ops:
  0.6 58.1 %shard_map.103 = (bf16[3,1280,256]{2,1,0:T(8,128)(2,1)S(1)}, bf16[3,2,2,64,256]{4,3,2,1,0:T(8,128)(2,1)S(1)}, bf16[1280,256]{1,0:T(8,128)(2,1)S(1)}, f32[3,64,256]{2,1,0:T(8,128)S(1)}, f32[3,64,256]{2,1,0:T(8,128)S(1)}) custom-call(bf16[4,1280,256]{2,1,0:T(8,128)(2,1)} %bitcast.21, bf16[4,1280,256]{2,1,0:T(8,128)(2,1)} %bitcast.22, ...), custom_call_target="tpu_custom_call" | custom-call | tf_op jit(solution)/shard_map/pallas_call | solution.py:954
  58.7 2.0 %shard_map.104 = (bf16[4,1280,256]{2,1,0:T(8,128)(2,1)}, f32[3,64,256]{2,1,0:T(8,128)}, f32[3,64,256]{2,1,0:T(8,128)}) custom-call(bf16[3,1280,256]{2,1,0:T(8,128)(2,1)S(1)} %get-tuple-element.11.done, bf16[3,2,2,64,256]{4,3,2,1,0:T(8,128)(2,1)S(1)} %get-tuple-element.12.usable, bf16[1280,256]{1,0:T(8,128)(2,1)S(1)} %get-tuple-element.13.asked, ...), custom_call_target="tpu_custom_call" | custom-call | tf_op jit(solution)/shard_map/pallas_call | solution.py:969

commit v6 on v5

--- a/solution.py
+++ b/solution.py
@@ -352,7 +352,7 @@
     k_hbm, v_hbm, q_hbm, rates_hbm, w_hbm, m_hbm, fw_hbm, fm_hbm,
     obuf, usable, asked_last, w_out, m_out,
     kbuf, vbuf, qbuf, kt, scaled, scaled_t, hid, bgu,
-    bank, gs, got, mid, tot, wst, mst,
+    bank, gs, got, mid, wst, mst,
     w_in, m_in, fw_in, fm_in, rates, mx, mr, msend, mrecv, sq,
     load_sem, in_sem, st_s, st_r, en_s, en_r, rl_s, rl_r, mm_s, mm_r, mx_s, mx_r, qs, qr,
 ):
@@ -374,10 +374,6 @@
 
     gather_to = (to_peer(1), to_peer(2))
     cross_to = (to_peer(2), to_peer(1))
-    own = (inner, outer)
-    far = (1 - inner, 1 - outer)
-    odd = lax.rem(seg, 2) == 1
-    even = jnp.logical_not(odd)
     down = {"seg": lax.rem(seg + 1, segs), "tok": tok}
     up = {"seg": lax.rem(seg + segs - 1, segs), "tok": tok}
 
@@ -452,11 +448,19 @@
             for d in (2, 3):
                 entry_copy(s, 0, d).wait_recv()
 
-    def moment_copies(s):
+    def moment_copies(s, targets):
         return [
             rcopy(mx.at[s], mr.at[s, tok], mx_s.at[d - 1], mx_r.at[s, d - 1], to_peer(d))
-            for d in (1, 2, 3)
+            for d in targets
         ]
+
+    def passed_moments(s):
+        strip = head // 8
+        copies = []
+        for d in (1, 2):
+            piece = mr.at[s, peers[3 - d], :, pl.ds((d - 1) * strip, strip), :]
+            copies.append(rcopy(piece, piece, mx_s.at[1 + d], mx_r.at[s, 1 + d], to_peer(d)))
+        return copies
 
     def square_copies():
         return [
@@ -480,7 +484,6 @@
         wst[2, outer, inner] = weights[1]
 
     def take_moments(s, moments):
-        arrive(moment_copies(s))
         for o in range(2):
             for i in range(2):
                 @pl.when(tok != 2 * o + i)
@@ -527,16 +530,6 @@
             st_s.at[item, p], st_r.at[lax.rem(b, 2), stage, item, p], (gather_to, cross_to)[stage][p],
         )
 
-    def trio_copy(b, stage, item, p):
-        if stage == 0:
-            src, dst, peer = gs.at[b, item, p, far[p]], got.at[b, 0, item, p, 0], gather_to[p]
-        elif stage == 1:
-            src, dst, peer = mid.at[b, item, p, 0], got.at[b, 1, item, p, 0], cross_to[p]
-        else:
-            src, peer = tot.at[b, item, p, own[p]], gather_to[p]
-            dst = src
-        return rcopy(src, dst, st_s.at[item, p], st_r.at[lax.rem(b, 2), stage, item, p], peer)
-
     def relay_copy(b, s, item):
         return rcopy(
             bank.at[b, item], bank.at[total + s + 1, item],
@@ -566,29 +559,16 @@
             bgu[c, at, :half] = (back * up_pre * slope).astype(bf16)
             bgu[c, at, half:] = (back * act).astype(bf16)
 
-    def send_grads(b, item):
+    def gradient(b, item):
         if item < 2:
             grad = mm(kt[...], bgu[item]).astype(bf16).T
         else:
             grad = mm(scaled_t[...], hid[...]).astype(bf16)
+        gs[b, item] = grad.reshape(gs.shape[2:])
+
+    def launch(b, item):
         for p in range(2):
-            gs[b, item, p] = grad[p * half:(p + 1) * half].reshape(gs.shape[3:])
-
-            @pl.when(jnp.logical_and(even, b > 0))
-            def _():
-                pair_copy(b - 1, 1, item, p).wait_send()
-
-            @pl.when(jnp.logical_and(odd, b > 0))
-            def _():
-                trio_copy(b - 1, 2, item, p).wait_send()
-
-            @pl.when(even)
-            def _():
-                pair_copy(b, 0, item, p).start()
-
-            @pl.when(odd)
-            def _():
-                trio_copy(b, 0, item, p).start()
+            pair_copy(b, 0, item, p).start()
 
     def pair_sum(b, item):
         for p in range(2):
@@ -596,22 +576,6 @@
             mid[b, item, p] = (gs[b, item, p].astype(f32) + got[b, 0, item, p].astype(f32)).astype(bf16)
             pair_copy(b, 0, item, p).wait_send()
             pair_copy(b, 1, item, p).start()
-
-    def trio_sum(b, item):
-        for p in range(2):
-            trio_copy(b, 0, item, p).wait_recv()
-            mine = gs[b, item, p, own[p]].astype(f32)
-            mid[b, item, p, 0] = (mine + got[b, 0, item, p, 0].astype(f32)).astype(bf16)
-            trio_copy(b, 0, item, p).wait_send()
-            trio_copy(b, 1, item, p).start()
-
-    def trio_cross(b, item):
-        for p in range(2):
-            trio_copy(b, 1, item, p).wait_recv()
-            both = mid[b, item, p, 0].astype(f32) + got[b, 1, item, p, 0].astype(f32)
-            tot[b, item, p, own[p]] = both.astype(bf16)
-            trio_copy(b, 1, item, p).wait_send()
-            trio_copy(b, 2, item, p).start()
 
     def step_half(b, item, p, factor, grad):
         moment = momentum_decay * mst[item, p] - grad * factor
@@ -632,18 +596,11 @@
             square = square + sq[p, s, pl.ds(g, 1), :]
         factor = lax.rsqrt(jnp.concatenate([square] * (head // LANES), axis=1))
 
-        @pl.when(even)
-        def _():
-            for p in range(2):
-                pair_copy(b, 1, item, p).wait_recv()
-                grad = mid[b, item, p].astype(f32) + got[b, 1, item, p].astype(f32)
-                step_half(b, item, p, factor, grad)
-
-        @pl.when(odd)
-        def _():
-            for p in range(2):
-                trio_copy(b, 2, item, p).wait_recv()
-                step_half(b, item, p, factor, tot[b, item, p].astype(f32))
+        for p in range(2):
+            pair_copy(b, 1, item, p).wait_recv()
+            pair_copy(b, 1, item, p).wait_send()
+            grad = mid[b, item, p].astype(f32) + got[b, 1, item, p].astype(f32)
+            step_half(b, item, p, factor, grad)
 
     def apply_fast(b, begin, stop):
         apply_tiles(begin, stop, tile, [matrix(b, item) for item in range(3)], qbuf.at[b], obuf.at[b])
@@ -654,7 +611,7 @@
     prepare_values(0)
     for j in range(2):
         entry_copy(0, j, 3).wait_send()
-    start(moment_copies(0))
+    start(moment_copies(0, (1, 2)))
     for copy in inputs[3:]:
         copy.wait()
     cut = (tiles + 1) // 2
@@ -684,7 +641,8 @@
                 relay_copy(b - 1, s - 1, item).wait_recv()
 
         flow(b, slot, 0)
-        send_grads(b, 0)
+        gradient(b, 0)
+        launch(b, 0)
 
         @pl.when(g > 0)
         def _():
@@ -699,8 +657,10 @@
             relay_copy(b - 1, s - 1, 1).wait_recv()
 
         flow(b, slot, 1)
-        send_grads(b, 2)
-        send_grads(b, 1)
+        gradient(b, 2)
+        launch(b, 2)
+        gradient(b, 1)
+        launch(b, 1)
 
         @pl.when(b == 0)
         def _():
@@ -711,43 +671,28 @@
         def _():
             prepare_keys(b + 1)
 
-        @pl.when(odd)
-        def _():
-            trio_sum(b, 0)
+        @pl.when(b == 0)
+        def _():
+            arrive(moment_copies(0, (1, 2)))
+            start(passed_moments(0))
 
         @pl.when(b > 0)
         def _():
             apply_fast(b - 1, 0, cut)
 
-        @pl.when(even)
-        def _():
-            pair_sum(b, 0)
-
-        @pl.when(odd)
-        def _():
-            trio_sum(b, 2)
-            trio_cross(b, 0)
+        pair_sum(b, 0)
 
         @pl.when(b > 0)
         def _():
             apply_fast(b - 1, cut, tiles)
 
-        @pl.when(even)
-        def _():
-            pair_sum(b, 2)
-
-        @pl.when(odd)
-        def _():
-            trio_sum(b, 1)
-            trio_cross(b, 2)
+        pair_sum(b, 2)
 
         @pl.when(b < total - 1)
         def _():
             prepare_values(b + 1)
 
-        @pl.when(even)
-        def _():
-            pair_sum(b, 1)
+        pair_sum(b, 1)
 
         for step in range(1, steps):
             @pl.when(jnp.logical_and(first, b == 0))
@@ -760,20 +705,23 @@
 
             @pl.when(jnp.logical_and(first, b == step * blocks - 1))
             def _():
-                for copy in moment_copies(step - 1):
+                sent = moment_copies(0, (1, 2)) + passed_moments(0)
+                for copy in sent if step == 1 else moment_copies(step - 1, (1, 2, 3)):
                     copy.wait_send()
                 mx[step] = fm_in[...].astype(bf16)
-                start(moment_copies(step))
+                start(moment_copies(step, (1, 2, 3)))
 
         @pl.when(b == 0)
         def _():
             arrive(square_copies())
             take_weights(0, w_in)
+            arrive(passed_moments(0))
             take_moments(0, m_in)
 
         @pl.when(renewed)
         def _():
             take_weights(s, fw_in)
+            arrive(moment_copies(s, (1, 2, 3)))
             take_moments(s, fm_in)
 
         @pl.when(entered)
@@ -792,10 +740,6 @@
                 relay_copy(b, s, item).start()
 
         finish(0)
-
-        @pl.when(odd)
-        def _():
-            trio_cross(b, 1)
 
         finish(2)
 
@@ -816,23 +760,20 @@
         ref[2] = state[outer, 1, inner]
         ref[1] = state[2, outer, inner]
 
-    def drain_entry(peers_left):
+    def drain_entry(peers_left, sent):
         for j in range(2):
             for d in peers_left:
                 entry_copy(0, j, d).wait_send()
-        for copy in moment_copies(0):
+        for copy in sent:
             copy.wait_send()
 
-    if steps > 1:
-        @pl.when(first)
-        def _():
-            drain_entry((1, 2, 3))
-
-        @pl.when(jnp.logical_not(first))
-        def _():
-            drain_entry((1, 2))
-    else:
-        drain_entry((1, 2))
+    @pl.when(first)
+    def _():
+        drain_entry((1, 2, 3), moment_copies(steps - 1, (1, 2, 3)))
+
+    @pl.when(jnp.logical_not(first))
+    def _():
+        drain_entry((1, 2), moment_copies(0, (1, 2)) + passed_moments(0))
 
     for copy in square_copies():
         copy.wait_send()
@@ -843,16 +784,6 @@
             for item in range(3):
                 relay_copy(s * blocks + blocks - 1, s, item).wait_send()
                 m_copy(s, item).wait_send()
-
-    for item in range(3):
-        for p in range(2):
-            @pl.when(even)
-            def _():
-                pair_copy(total - 1, 1, item, p).wait_send()
-
-            @pl.when(odd)
-            def _():
-                trio_copy(total - 1, 2, item, p).wait_send()
 
 
 def tail_kernel(
@@ -898,7 +829,6 @@
         vmem((total, 3) + whole, bf16),
         vmem((total, 2, 3) + whole, bf16),
         vmem((total, 3) + whole, bf16),
-        vmem((total, 3) + whole, bf16),
         vmem((3,) + whole, f32),
         vmem((3,) + whole, f32),
         vmem(piece, f32),
@@ -914,15 +844,15 @@
         dma((6,)),
         dma((5,)),
         dma((3, 2)),
-        dma((2, 3, 3, 2)),
+        dma((2, 2, 3, 2)),
         dma((3, 2)),
         dma((steps, 3, 2)),
         dma((steps - 1, 3)),
         dma((steps - 1, 3)),
         dma((steps - 1, 3)),
         dma((steps - 1, 3)),
-        dma((3,)),
-        dma((steps, 3)),
+        dma((4,)),
+        dma((steps, 4)),
         dma((3,)),
         dma((3,)),
     ]

time: 60.8 us -> 59.1 us (0.972)
  the two profiles are of different devices: /device:TPU:1 before, /device:TPU:0 now
where the time goes in v6:
time: 59.1 us; the launch traced here: 59 us
  Pallas kernels  58.3 us (99%)
  between operations  0.64 us (1%)
    pallas_call x1, Pallas kernels, body(): pl.pallas_call(functools.partial(quad_kernel, segs, steps, blocks, tile),...  56.3 us
    pallas_call x1, Pallas kernels, body(): pl.pallas_call(functools.partial(tail_kernel, tile), out_shape=results, i...  1.98 us

profile of v6, /device:TPU:0, one launch (start us, length us, event | category | flops | bytes accessed | tf_op | source)
XLA Modules:
  0.0 59.0 jit_solution(3433355649360228402)
XLA Ops:
  0.6 56.3 %shard_map.103 = (bf16[3,1280,256]{2,1,0:T(8,128)(2,1)S(1)}, bf16[3,2,2,64,256]{4,3,2,1,0:T(8,128)(2,1)S(1)}, bf16[1280,256]{1,0:T(8,128)(2,1)S(1)}, f32[3,64,256]{2,1,0:T(8,128)S(1)}, f32[3,64,256]{2,1,0:T(8,128)S(1)}) custom-call(bf16[4,1280,256]{2,1,0:T(8,128)(2,1)} %bitcast.21, bf16[4,1280,256]{2,1,0:T(8,128)(2,1)} %bitcast.22, ...), custom_call_target="tpu_custom_call" | custom-call | tf_op jit(solution)/shard_map/pallas_call | solution.py:884
  57.0 2.0 %shard_map.104 = (bf16[4,1280,256]{2,1,0:T(8,128)(2,1)}, f32[3,64,256]{2,1,0:T(8,128)}, f32[3,64,256]{2,1,0:T(8,128)}) custom-call(bf16[3,1280,256]{2,1,0:T(8,128)(2,1)S(1)} %get-tuple-element.11.done, bf16[3,2,2,64,256]{4,3,2,1,0:T(8,128)(2,1)S(1)} %get-tuple-element.12.usable, bf16[1280,256]{1,0:T(8,128)(2,1)S(1)} %get-tuple-element.13.asked, ...), custom_call_target="tpu_custom_call" | custom-call | tf_op jit(solution)/shard_map/pallas_call | solution.py:899

commit v7 on v6

--- a/solution.py
+++ b/solution.py
@@ -332,25 +332,26 @@
         pltpu.make_async_copy(obuf.at[b], out_hbm.at[b], store_sem.at[b]).wait()
 
 
+def gated(asked, w13):
+    both = mm_t(asked, w13)
+    half = both.shape[1] // 2
+    gate = both[:, :half]
+    return (gate * sigmoid(gate) * both[:, half:]).astype(bf16)
+
+
 def apply_tiles(begin, stop, tile, weights, asked_ref, out_ref):
-    half = asked_ref.shape[-1] // 2
-
     @pl.loop(begin, stop, unroll=min(UNROLL, stop - begin))
     def _(i):
         at = pl.ds(pl.multiple_of(i * tile, tile), tile)
         asked = asked_ref[at, :]
-        parts = []
-        for w13 in weights[:2]:
-            both = mm_t(asked, w13)
-            gate = both[:, :half]
-            parts.append((gate * sigmoid(gate) * both[:, half:]).astype(bf16))
+        parts = [gated(asked, w13) for w13 in weights[:2]]
         out_ref[at, :] = mm_t(jnp.concatenate(parts, axis=1), weights[2]).astype(bf16)
 
 
 def quad_kernel(
     segs, steps, blocks, tile,
     k_hbm, v_hbm, q_hbm, rates_hbm, w_hbm, m_hbm, fw_hbm, fm_hbm,
-    obuf, usable, asked_last, w_out, m_out,
+    obuf, usable, asked_last, begun, w_out, m_out,
     kbuf, vbuf, qbuf, kt, scaled, scaled_t, hid, bgu,
     bank, gs, got, mid, wst, mst,
     w_in, m_in, fw_in, fm_in, rates, mx, mr, msend, mrecv, sq,
@@ -741,6 +742,17 @@
 
         finish(0)
 
+        @pl.when(b == total - 1)
+        def _():
+            later[3].wait()
+            w13 = matrix(b, 0)
+
+            @pl.loop(0, tiles, unroll=UNROLL)
+            def _(i):
+                at = pl.ds(pl.multiple_of(i * tile, tile), tile)
+                begun[at, :] = gated(asked_last[at, :], w13)
+
+
         finish(2)
 
         @pl.when(g == blocks - 1)
@@ -754,7 +766,6 @@
                 m_copy(s, item).start()
 
     usable[...] = bank[total - 1]
-    later[3].wait()
     for ref, state in ((w_out, wst), (m_out, mst)):
         ref[0] = state[outer, 0, inner]
         ref[2] = state[outer, 1, inner]
@@ -787,7 +798,7 @@
 
 
 def tail_kernel(
-    tile, done, usable, asked, w_ready, m_ready, out_hbm, w_hbm, m_hbm, obuf, sem,
+    tile, done, usable, asked, begun, w_ready, m_ready, out_hbm, w_hbm, m_hbm, obuf, sem,
 ):
     count = done.shape[0]
     rows, head = asked.shape
@@ -801,8 +812,9 @@
         copy.start()
     weights = [usable[item].reshape(head, head) for item in range(3)]
     for i in range(rows // tile):
-        apply_tiles(i, i + 1, tile, weights, asked, obuf)
         at = pl.ds(i * tile, tile)
+        hidden = jnp.concatenate([begun[at, :], gated(asked[at, :], weights[1])], axis=1)
+        obuf[at, :] = mm_t(hidden, weights[2]).astype(bf16)
         copy = pltpu.make_async_copy(obuf.at[at], out_hbm.at[count, at], sem.at[count + 2 + i])
         copy.start()
         copies.append(copy)
@@ -887,10 +899,11 @@
                 jax.ShapeDtypeStruct((total - 1, rows, head), bf16),
                 jax.ShapeDtypeStruct((3, 2, 2, head // 4, head), bf16),
                 jax.ShapeDtypeStruct(big, bf16),
+                jax.ShapeDtypeStruct((rows, head // 2), bf16),
                 *results[1:],
             ),
             in_specs=[pl.BlockSpec(memory_space=pltpu.HBM)] * 8,
-            out_specs=(vmem,) * 5,
+            out_specs=(vmem,) * 6,
             scratch_shapes=quad_scratch(steps, blocks, rows, head),
             compiler_params=pltpu.CompilerParams(
                 collective_id=0, has_side_effects=True, vmem_limit_bytes=QUAD_VMEM
@@ -899,7 +912,7 @@
         outs = pl.pallas_call(
             functools.partial(tail_kernel, tile),
             out_shape=results,
-            in_specs=[vmem] * 5,
+            in_specs=[vmem] * 6,
             out_specs=(hbm,) * 3,
             scratch_shapes=[pltpu.VMEM(big, bf16), dma((total + 1 + rows // tile,))],
             compiler_params=pltpu.CompilerParams(vmem_limit_bytes=16 * 1024 * 1024),

time: 59.1 us -> 58.8 us (level)
  no operation moved by 1% of the time
where the time goes in v7:
time: 58.8 us; the launch traced here: 58.7 us
  Pallas kernels  58.1 us (99%)
  between operations  0.64 us (1%)
    pallas_call x1, Pallas kernels, body(): pl.pallas_call(functools.partial(quad_kernel, segs, steps, blocks, tile),...  56.4 us
    pallas_call x1, Pallas kernels, body(): pl.pallas_call(functools.partial(tail_kernel, tile), out_shape=results, i...  1.7 us

profile of v7, /device:TPU:0, one launch (start us, length us, event | category | flops | bytes accessed | tf_op | source)
XLA Modules:
  0.0 58.7 jit_solution(15095992484144604836)
XLA Ops:
  0.6 56.4 %shard_map.103 = (bf16[3,1280,256]{2,1,0:T(8,128)(2,1)S(1)}, bf16[3,2,2,64,256]{4,3,2,1,0:T(8,128)(2,1)S(1)}, bf16[1280,256]{1,0:T(8,128)(2,1)S(1)}, bf16[1280,1...) custom-call(bf16[4,1280,256]{2,1,0:T(8,128)(2,1)} %bitcast.21, ...), custom_call_target="tpu_custom_call" | custom-call | tf_op jit(solution)/shard_map/pallas_call | solution.py:896
  57.0 1.7 %shard_map.104 = (bf16[4,1280,256]{2,1,0:T(8,128)(2,1)}, f32[3,64,256]{2,1,0:T(8,128)}, f32[3,64,256]{2,1,0:T(8,128)}) custom-call(bf16[3,1280,256]{2,1,0:T(8,128)(2,1)S(1)} %get-tuple-element.12.done, bf16[3,2,2,64,256]{4,3,2,1,0:T(8,128)(2,1)S(1)} %get-tuple-element.13.usable, bf16[1280,256]{1,0:T(8,128)(2,1)S(1)} %get-tuple-element.14.asked, ...), custom_call_target="tpu_custom_call" | custom-call | tf_op jit(solution)/shard_map/pallas_call | solution.py:912

commit v8 on v7

--- a/solution.py
+++ b/solution.py
@@ -537,8 +537,8 @@
             rl_s.at[s, item], rl_r.at[s, item], down,
         )
 
-    def m_copy(s, item):
-        return rcopy(msend.at[s, item], mrecv.at[s, item], mm_s.at[s, item], mm_r.at[s, item], down)
+    def m_copy(s):
+        return rcopy(msend.at[s], mrecv.at[s], mm_s.at[s], mm_r.at[s], down)
 
     def matrix(slot, item):
         return bank[slot, item].reshape(head, head)
@@ -729,8 +729,8 @@
         def _():
             for item in range(3):
                 wst[item] = bank[total + s, item].astype(f32)
+            m_copy(s - 1).wait_recv()
             for item in range(3):
-                m_copy(s - 1, item).wait_recv()
                 mst[item] = mrecv[s - 1, item].astype(f32)
 
         def finish(item):
@@ -763,7 +763,7 @@
         def _():
             for item in (0, 2, 1):
                 msend[s, item] = mst[item].astype(bf16)
-                m_copy(s, item).start()
+            m_copy(s).start()
 
     usable[...] = bank[total - 1]
     for ref, state in ((w_out, wst), (m_out, mst)):
@@ -794,7 +794,7 @@
         for s in range(steps - 1):
             for item in range(3):
                 relay_copy(s * blocks + blocks - 1, s, item).wait_send()
-                m_copy(s, item).wait_send()
+            m_copy(s).wait_send()
 
 
 def tail_kernel(
@@ -861,8 +861,8 @@
         dma((steps, 3, 2)),
         dma((steps - 1, 3)),
         dma((steps - 1, 3)),
-        dma((steps - 1, 3)),
-        dma((steps - 1, 3)),
+        dma((steps - 1,)),
+        dma((steps - 1,)),
         dma((4,)),
         dma((steps, 4)),
         dma((3,)),

time: 58.8 us -> 58.8 us (level)
  no operation moved by 1% of the time
where the time goes in v8:
time: 58.8 us; the launch traced here: 58.7 us
  Pallas kernels  58 us (99%)
  between operations  0.64 us (1%)
    pallas_call x1, Pallas kernels, body(): pl.pallas_call(functools.partial(quad_kernel, segs, steps, blocks, tile),...  56.3 us
    pallas_call x1, Pallas kernels, body(): pl.pallas_call(functools.partial(tail_kernel, tile), out_shape=results, i...  1.7 us

profile of v8, /device:TPU:0, one launch (start us, length us, event | category | flops | bytes accessed | tf_op | source)
XLA Modules:
  0.0 58.7 jit_solution(1488928502510932438)
XLA Ops:
  0.6 56.3 %shard_map.103 = (bf16[3,1280,256]{2,1,0:T(8,128)(2,1)S(1)}, bf16[3,2,2,64,256]{4,3,2,1,0:T(8,128)(2,1)S(1)}, bf16[1280,256]{1,0:T(8,128)(2,1)S(1)}, bf16[1280,1...) custom-call(bf16[4,1280,256]{2,1,0:T(8,128)(2,1)} %bitcast.21, ...), custom_call_target="tpu_custom_call" | custom-call | tf_op jit(solution)/shard_map/pallas_call | solution.py:896
  57.0 1.7 %shard_map.104 = (bf16[4,1280,256]{2,1,0:T(8,128)(2,1)}, f32[3,64,256]{2,1,0:T(8,128)}, f32[3,64,256]{2,1,0:T(8,128)}) custom-call(bf16[3,1280,256]{2,1,0:T(8,128)(2,1)S(1)} %get-tuple-element.12.done, bf16[3,2,2,64,256]{4,3,2,1,0:T(8,128)(2,1)S(1)} %get-tuple-element.13.usable, bf16[1280,256]{1,0:T(8,128)(2,1)S(1)} %get-tuple-element.14.asked, ...), custom_call_target="tpu_custom_call" | custom-call | tf_op jit(solution)/shard_map/pallas_call | solution.py:912
